TPU v7x, 256 devices: a whole 4x4x8 slice. The times are simulated.
256 devices in a mesh: tm: 32 (over z, y_hi, core), space: 8 (over x, y_lo).
Axes of the slice: x: 4, y: 4 (y_hi: 2, y_lo: 2; y = y_hi * 2 + y_lo), z: 8, core: 2. Of those that a mesh axis runs over, the one named last changes fastest.
Arguments:
- start_states: float32 [32, 3, 16, 256, 256], P('tm', None, 'space'), may hold values from -6 to 6
- wall_normal: bfloat16 [256, 256], replicated, may hold values from -0.375 to 0.375
- spanwise: bfloat16 [256, 256], replicated, may hold values from -0.375 to 0.375
- base_flow: float32 [3, 256], replicated, may hold values from -1.5 to 1.5
Outputs:
- end_state: float32 [32, 3, 16, 256, 256], P('tm', None, 'space')
All inputs are finite; a program needn't handle non-finite values.
Results may differ from a plain program's by a relative error of at most 0.0017.
Values sent between devices are 32-bit elements; how exact they have to be, the bound alone decides.
No kernel may reach another device: no remote copies, remote signals or barrier semaphores. Data moves between devices by JAX's collectives and lax.ppermute only.
A program may use at most 64 MiB of HBM per device.

v0:
```python
import jax
import jax.numpy as jnp
from jax import lax
from jax.sharding import PartitionSpec as P

TICKS = 2


step_size = 0.2


def padded_2(cells, sides, width):
    for axis, dim in sides:
        count = lax.axis_size(axis)
        head = lax.slice_in_dim(cells, 0, width, axis=dim)
        tail = lax.slice_in_dim(cells, cells.shape[dim] - width, cells.shape[dim], axis=dim)
        cells = jnp.concatenate(
            [
                lax.ppermute(tail, axis, [(i, (i + 1) % count) for i in range(count)]),
                cells,
                lax.ppermute(head, axis, [((i + 1) % count, i) for i in range(count)]),
            ],
            axis=dim,
        )
    return cells


def shifted(array, axis, by):
    length = lax.axis_size(axis)
    pairs = [(i, i + by) for i in range(length) if 0 <= i + by < length]
    return lax.ppermute(array, axis, pairs)


def tendency(padded, wall_normal, spanwise, base_flow):
    inner = padded[:, 1:-1]
    grad_x = 0.5 * (padded[:, 2:] - padded[:, :-2])
    rounded = inner.astype(jnp.bfloat16)
    grad_y = jnp.einsum("yk,cxkz->cxyz", wall_normal, rounded, preferred_element_type=jnp.float32)
    width = rounded.shape[-1]
    grad_z = jnp.dot(
        rounded.reshape(-1, width), spanwise, preferred_element_type=jnp.float32
    ).reshape(inner.shape)
    velocity = base_flow[:, None, :, None] + inner
    return -(velocity[0:1] * grad_x + velocity[1:2] * grad_y + velocity[2:3] * grad_z)


def local(start_states, wall_normal, spanwise, base_flow):
    begin = start_states[0]
    leading = lax.axis_index("tm") == 0
    begin_wide = padded_2(begin, (("space", 1),), 1)
    finish = begin
    finish_wide = begin_wide
    old_rate = tendency(begin_wide, wall_normal, spanwise, base_flow)
    fresh = old_rate
    for tick in range(TICKS):
        final = tick == TICKS - 1
        if tick > 0:
            fresh = tendency(begin_wide, wall_normal, spanwise, base_flow)
        end_rate = tendency(finish_wide, wall_normal, spanwise, base_flow)
        finish = begin + step_size * (fresh - old_rate) + 0.5 * step_size * (old_rate + end_rate)
        old_rate = fresh
        if not final:
            moved = shifted(finish, "tm", 1)
            begin = jnp.where(leading, begin, moved)
            begin_wide, finish_wide = (
                padded_2(begin, (("space", 1),), 1),
                padded_2(finish, (("space", 1),), 1),
            )
    return finish[None]


def solution(mesh):
    placed = (P("tm", None, "space", None, None), P(), P(), P())
    return jax.shard_map(
        local,
        mesh=mesh,
        in_specs=placed,
        out_specs=P("tm", None, "space", None, None),
        check_vma=False,
    )
```

profile of v0, /device:TPU:113, one launch (start us, length us, event | category | flops | bytes accessed | tf_op | source)
XLA Modules:
  0.0 134.9 jit_solution(2340846915274270857)
XLA Ops:
  0.0 1.9 %copy.5 = f32[1,3,2,256,256]{3,4,2,1,0:T(8,128)S(1)} copy(f32[1,3,2,256,256]{4,3,2,1,0:T(8,128)} %param.4) | data formatting | bytes 3145728 | tf_op args[0]
  1.9 0.0 copy-start.4
  1.9 0.2 fusion.45
  2.1 3.3 %collective-permute-start = (f32[3,1,256,256]{2,3,1,0:T(8,128)S(1)}, f32[3,1,256,256]{2,3,1,0:T(8,128)S(1)}, u32[]{:S(2)}, u32[]{:S(2)}) collective-permute-start(f32[3,1,256,256]{2,3,1,0:T(8,128)S(1)} %get-tuple-element.22), channel_id=1, source_target_pairs={{1,0},{2,1},{3,2},{4,3},{5,4},{6,5},{7,6},{0,7},{9,8},{10,9},{11,1... | collective-permute-start | bytes 2359304 | tf_op jit(solution)/shard_map/ppermute | solution.py:21
  5.4 0.0 collective-permute-start.1
  5.4 0.2 broadcast_add_fusion.2
  5.6 0.0 copy-start.3
  5.6 0.1 fusion.24
  5.7 0.7 copy-done.3
  6.5 0.4 fusion.32
  6.9 30.6 %collective-permute-done = f32[3,1,256,256]{2,3,1,0:T(8,128)S(1)} collective-permute-done((f32[3,1,256,256]{2,3,1,0:T(8,128)S(1)}, f32[3,1,256,256]{2,3,1,0:T(8,128)S(1)}, u32[]{:S(2)}, u32[]{:S(2)}) %collective-permute-start) | collective-permute-done | bytes 786464 | tf_op jit(solution)/shard_map/ppermute | solution.py:21
  37.5 0.7 collective-permute-done.1
  38.2 2.7 %broadcast_add_fusion = (f32[3,2,256,256]{2,3,1,0:T(8,128)}, f32[3,2,256,256]{2,3,1,0:T(8,128)S(1)}, f32[3,2,256,256]{2,3,1,0:T(8,128)}) fusion(f32[3,256]{1,0:T(4,128)S(1)} %copy-done.4, f32[1,3,2,256,256]{3,4,2,1,0:T(8,128)S(1)} %copy.5, f32[3,2,256,256]{2,3,1,0:T(8,128)S(1)} %fusion.32, f32[2,256,256]{1,2,0:T(8,128)S(1)} %get-tuple-element.20, ...), kind=kOutput, calls=%fused_computation.32 | convolution fusion | flops 208011264 | bytes 12717056 | tf_op jit(solution)/shard_map/yk,cxkz->cxyz/dot_general | solution.py:38
  40.9 5.2 %collective-permute-start.2 = (f32[3,2,256,256]{2,3,1,0:T(8,128)S(1)}, f32[3,2,256,256]{2,3,1,0:T(8,128)}, u32[]{:S(2)}, u32[]{:S(2)}) collective-permute-start(f32[3,2,256,256]{2,3,1,0:T(8,128)S(1)} %get-tuple-element.8), channel_id=1, source_target_pairs={{0,8},{8,16},{16,24},{24,32},{32,40},{40,48},{48,56},{56,64},{64,7... | collective-permute-start | bytes 4718600 | tf_op jit(solution)/shard_map/ppermute | solution.py:31
  46.1 0.0 copy-start.2
  46.1 0.2 fusion.44
  46.3 4.4 %collective-permute-start.5 = (f32[3,1,256,256]{2,3,1,0:T(8,128)S(1)}, f32[3,1,256,256]{2,3,1,0:T(8,128)S(1)}, u32[]{:S(2)}, u32[]{:S(2)}) collective-permute-start(f32[3,1,256,256]{2,3,1,0:T(8,128)S(1)} %get-tuple-element.17), channel_id=1, source_target_pairs={{1,0},{2,1},{3,2},{4,3},{5,4},{6,5},{7,6},{0,7},{9,8},{10,9},{11,1... | collective-permute-start | bytes 2359304 | tf_op jit(solution)/shard_map/ppermute | solution.py:21
  50.7 0.0 collective-permute-start.6
  50.7 0.1 fusion.22
  50.9 0.4 fusion.25
  51.3 21.1 %collective-permute-done.2 = f32[3,2,256,256]{2,3,1,0:T(8,128)} collective-permute-done((f32[3,2,256,256]{2,3,1,0:T(8,128)S(1)}, f32[3,2,256,256]{2,3,1,0:T(8,128)}, u32[]{:S(2)}, u32[]{:S(2)}) %collective-permute-start.2) | collective-permute-done | bytes 1572896 | tf_op jit(solution)/shard_map/ppermute | solution.py:31
  72.4 1.6 %broadcast_add_fusion.1 = (f32[3,2,256,256]{2,3,1,0:T(8,128)S(1)}, f32[3,2,256,256]{2,3,1,0:T(8,128)S(1)}) fusion(f32[3,256]{1,0:T(4,128)S(1)} %copy-done.4, f32[3,2,256,256]{2,3,1,0:T(8,128)} %collective-permute-done.2, f32[1,3,2,256,256]{3,4,2,1,0:T(8,128)S(1)} %copy.5, pred[]{:T(512)S(6)} %eq.3), kind=kLoop, calls=%fused_computation.33 | loop fusion | flops 786432 | bytes 6294529 | tf_op jit(solution)/shard_map/add | solution.py:43
  74.0 0.1 fusion.43
  74.1 4.9 %collective-permute-start.3 = (f32[3,1,256,256]{2,3,1,0:T(8,128)S(1)}, f32[3,1,256,256]{2,3,1,0:T(8,128)S(1)}, u32[]{:S(2)}, u32[]{:S(2)}) collective-permute-start(f32[3,1,256,256]{2,3,1,0:T(8,128)S(1)} %get-tuple-element.15), channel_id=1, source_target_pairs={{1,0},{2,1},{3,2},{4,3},{5,4},{6,5},{7,6},{0,7},{9,8},{10,9},{11,1... | collective-permute-start | bytes 2359304 | tf_op jit(solution)/shard_map/ppermute | solution.py:21
  79.0 0.5 collective-permute-start.4
  79.5 0.1 fusion.23
  79.6 0.4 fusion.30
  80.0 0.4 fusion.28
  80.4 27.1 %collective-permute-done.5 = f32[3,1,256,256]{2,3,1,0:T(8,128)S(1)} collective-permute-done((f32[3,1,256,256]{2,3,1,0:T(8,128)S(1)}, f32[3,1,256,256]{2,3,1,0:T(8,128)S(1)}, u32[]{:S(2)}, u32[]{:S(2)}) %collective-permute-start.5) | collective-permute-done | bytes 786464 | tf_op jit(solution)/shard_map/ppermute | solution.py:21
  107.5 23.6 %collective-permute-done.3 = f32[3,1,256,256]{2,3,1,0:T(8,128)S(1)} collective-permute-done((f32[3,1,256,256]{2,3,1,0:T(8,128)S(1)}, f32[3,1,256,256]{2,3,1,0:T(8,128)S(1)}, u32[]{:S(2)}, u32[]{:S(2)}) %collective-permute-start.3) | collective-permute-done | bytes 786464 | tf_op jit(solution)/shard_map/ppermute | solution.py:21
  131.2 2.1 %fusion.8 = f32[1,3,2,256,256]{3,4,2,1,0:T(8,128)S(1)} fusion(f32[3,2,256,256]{2,3,1,0:T(8,128)S(1)} %copy-done.1, f32[3,2,256,256]{2,3,1,0:T(8,128)S(1)} %get-tuple-element.8, f32[3,1,256,256]{2,3,1,0:T(8,128)S(1)} %collective-permute-done.6, f32[3,1,256,256]{2,3,1,0:T(8,128)S(1)} %collective-permute-done.5, f32[3,2,256,256]{2,3,1,0:T(8,128)S(1)} %get-tuple-element.6, ...), kind=kOutput, calls=%fused_computation.9 | convolution fusion | flops 211156992 | bytes 17432576 | tf_op jit(solution)/shard_map/yk,cxkz->cxyz/dot_general | solution.py:38
  133.3 1.6 %copy.12 = f32[1,3,2,256,256]{4,3,2,1,0:T(8,128)} copy(f32[1,3,2,256,256]{3,4,2,1,0:T(8,128)S(1)} %fusion.8) | data formatting | bytes 3145728 | tf_op jit(solution)/shard_map/broadcast_in_dim | solution.py:69
  (8 shorter events, 0.0 us)
Async XLA Ops:
  0.0 38.2 %copy-start = (bf16[256,256]{1,0:T(8,128)(2,1)S(1)}, bf16[256,256]{1,0:T(8,128)(2,1)}, u32[]{:S(2)}) copy-start(bf16[256,256]{1,0:T(8,128)(2,1)} %param.5) | copy-start | bytes 393220
  1.9 3.5 %copy-start.4 = (f32[3,256]{1,0:T(4,128)S(1)}, f32[3,256]{1,0:T(4,128)}, u32[]{:S(2)}) copy-start(f32[3,256]{1,0:T(4,128)} %param.7) | copy-start | bytes 9220
  2.1 35.4 %collective-permute-start = (f32[3,1,256,256]{2,3,1,0:T(8,128)S(1)}, f32[3,1,256,256]{2,3,1,0:T(8,128)S(1)}, u32[]{:S(2)}, u32[]{:S(2)}) collective-permute-start(f32[3,1,256,256]{2,3,1,0:T(8,128)S(1)} %get-tuple-element.22), channel_id=1, source_target_pairs={{1,0},{2,1},{3,2},{4,3},{5,4},{6,5},{7,6},{0,7},{9,8},{10,9},{11,1... | collective-permute-start | bytes 2359304 | tf_op jit(solution)/shard_map/ppermute | solution.py:21
  5.4 32.8 %collective-permute-start.1 = (f32[3,1,256,256]{2,3,1,0:T(8,128)S(1)}, f32[3,1,256,256]{2,3,1,0:T(8,128)S(1)}, u32[]{:S(2)}, u32[]{:S(2)}) collective-permute-start(f32[3,1,256,256]{2,3,1,0:T(8,128)S(1)} %get-tuple-element.23), channel_id=1, source_target_pairs={{0,1},{1,2},{2,3},{3,4},{4,5},{5,6},{6,7},{7,0},{8,9},{9,10},{10,1... | collective-permute-start | bytes 2359304 | tf_op jit(solution)/shard_map/ppermute | solution.py:19
  5.6 0.9 copy-start.3
  40.9 31.5 %collective-permute-start.2 = (f32[3,2,256,256]{2,3,1,0:T(8,128)S(1)}, f32[3,2,256,256]{2,3,1,0:T(8,128)}, u32[]{:S(2)}, u32[]{:S(2)}) collective-permute-start(f32[3,2,256,256]{2,3,1,0:T(8,128)S(1)} %get-tuple-element.8), channel_id=1, source_target_pairs={{0,8},{8,16},{16,24},{24,32},{32,40},{40,48},{48,56},{56,64},{64,7... | collective-permute-start | bytes 4718600 | tf_op jit(solution)/shard_map/ppermute | solution.py:31
  46.1 4.6 %copy-start.2 = (f32[3,2,256,256]{2,3,1,0:T(8,128)S(1)}, f32[3,2,256,256]{2,3,1,0:T(8,128)}, u32[]{:S(2)}) copy-start(f32[3,2,256,256]{2,3,1,0:T(8,128)} %get-tuple-element.7) | copy-start | bytes 4718596
  46.3 61.2 %collective-permute-start.5 = (f32[3,1,256,256]{2,3,1,0:T(8,128)S(1)}, f32[3,1,256,256]{2,3,1,0:T(8,128)S(1)}, u32[]{:S(2)}, u32[]{:S(2)}) collective-permute-start(f32[3,1,256,256]{2,3,1,0:T(8,128)S(1)} %get-tuple-element.17), channel_id=1, source_target_pairs={{1,0},{2,1},{3,2},{4,3},{5,4},{6,5},{7,6},{0,7},{9,8},{10,9},{11,1... | collective-permute-start | bytes 2359304 | tf_op jit(solution)/shard_map/ppermute | solution.py:21
  50.7 56.8 %collective-permute-start.6 = (f32[3,1,256,256]{2,3,1,0:T(8,128)S(1)}, f32[3,1,256,256]{2,3,1,0:T(8,128)S(1)}, u32[]{:S(2)}, u32[]{:S(2)}) collective-permute-start(f32[3,1,256,256]{2,3,1,0:T(8,128)S(1)} %get-tuple-element.18), channel_id=1, source_target_pairs={{0,1},{1,2},{2,3},{3,4},{4,5},{5,6},{6,7},{7,0},{8,9},{9,10},{10,1... | collective-permute-start | bytes 2359304 | tf_op jit(solution)/shard_map/ppermute | solution.py:19
  74.1 57.0 %collective-permute-start.3 = (f32[3,1,256,256]{2,3,1,0:T(8,128)S(1)}, f32[3,1,256,256]{2,3,1,0:T(8,128)S(1)}, u32[]{:S(2)}, u32[]{:S(2)}) collective-permute-start(f32[3,1,256,256]{2,3,1,0:T(8,128)S(1)} %get-tuple-element.15), channel_id=1, source_target_pairs={{1,0},{2,1},{3,2},{4,3},{5,4},{6,5},{7,6},{0,7},{9,8},{10,9},{11,1... | collective-permute-start | bytes 2359304 | tf_op jit(solution)/shard_map/ppermute | solution.py:21
  79.0 52.2 %collective-permute-start.4 = (f32[3,1,256,256]{2,3,1,0:T(8,128)S(1)}, f32[3,1,256,256]{2,3,1,0:T(8,128)S(1)}, u32[]{:S(2)}, u32[]{:S(2)}) collective-permute-start(f32[3,1,256,256]{2,3,1,0:T(8,128)S(1)} %get-tuple-element.16), channel_id=1, source_target_pairs={{0,1},{1,2},{2,3},{3,4},{4,5},{5,6},{6,7},{7,0},{8,9},{9,10},{10,1... | collective-permute-start | bytes 2359304 | tf_op jit(solution)/shard_map/ppermute | solution.py:19
  80.0 51.2 %copy-start.1 = (f32[3,2,256,256]{2,3,1,0:T(8,128)S(1)}, f32[3,2,256,256]{2,3,1,0:T(8,128)}, u32[]{:S(2)}) copy-start(f32[3,2,256,256]{2,3,1,0:T(8,128)} %get-tuple-element.24) | copy-start | bytes 4718596
where the time goes:
time: 137 us; the launch traced here: 135 us
  waiting for transfers between devices  103 us (75%)
  starting transfers between devices  18.3 us (13%)
  matrix products  6.41 us (5%)
  local copies, waits for them, and re-layouts  4.75 us (3%)
  other arithmetic  2.16 us (2%)
    ppermute x3, waiting for transfers between devices, padded_2(): lax.ppermute(head, axis, [((i + 1) % count, i) for i in range(count)])  81.3 us
    ppermute x1, waiting for transfers between devices, shifted(): return lax.ppermute(array, axis, pairs)  21.1 us
    ppermute x3, starting transfers between devices, padded_2(): lax.ppermute(head, axis, [((i + 1) % count, i) for i in range(count)])  12.6 us
    ppermute x1, starting transfers between devices, shifted(): return lax.ppermute(array, axis, pairs)  5.2 us
    dot_general x3, matrix products, tendency(): jnp.einsum('yk,cxkz->cxyz', wall_normal, rounded, preferred_element_type=...  5.16 us
  transfers between devices with their start and end apart: 7, of which 5 were waited for; matrix products, arithmetic and copies ran while one was open for 3% of the time, Pallas kernels for 0%

commit v1 on v0

v1 whole, which is shorter than its diff:
```python
import functools

import jax
import jax.numpy as jnp
from jax import lax
from jax.experimental import pallas as pl
from jax.experimental.pallas import tpu as pltpu
from jax.sharding import PartitionSpec as P

AXES = ("tm", "space")
STEP = 0.2


def routes(slices, slabs):
    at = lambda s, p: s * slabs + p % slabs
    cells = [(k, x, l) for k in range(slices // 2) for x in range(slabs // 2) for l in range(2)]
    side = lambda l: 1 - 2 * l
    stay = lambda k, x, l: at(2 * k + l, 2 * x + l)
    move = lambda k, x, l: at(2 * k + 1 - l, 2 * x + l)
    return {
        "swap": [(move(k, x, l), move(k, x, 1 - l)) for k, x, l in cells],
        "near_in": [(stay(k, x, l), move(k, x, l)) for k, x, l in cells],
        "far_in": [(stay(k, x + side(l), l), move(k, x, l)) for k, x, l in cells],
        "near_out": [(move(k, x, l), stay(k, x, l)) for k, x, l in cells],
        "far_out": [(move(k, x, l), stay(k, x + side(l), l)) for k, x, l in cells],
        "next_move": [
            (move(k, x, l), at(2 * k + l + 1, 2 * x + 1 - l)) for k, x, l in cells if 2 * k + l + 1 < slices
        ],
        "next_stay": [(stay(k, x, l), at(2 * k + l + 1, 2 * x + l)) for k, x, l in cells if 2 * k + l + 1 < slices],
    }


def advance(flags, near, own, far, wall, span, flow, a_ref, b_ref, mid):
    low = flags[0]
    sign = jnp.where(low == 1, 0.5, -0.5).astype(jnp.float32)
    first = jnp.where(flags[1] == 1, 1.0, 0.0).astype(jnp.float32)
    one = lambda i: jnp.where(low == 1, i, 1 - i)
    order = [(near, one(0)), (near, one(1)), (own, one(0)), (own, one(1)), (far, one(0)), (far, one(1))]

    def rate(before, here, after):
        fields = [here(c) for c in range(3)]
        vel = [flow[c] + fields[c] for c in range(3)]
        vx = vel[0] * sign
        out = []
        for c in range(3):
            rounded = fields[c].astype(jnp.bfloat16)
            gy = jnp.dot(wall[...], rounded, preferred_element_type=jnp.float32)
            gz = jnp.dot(rounded, span[...], preferred_element_type=jnp.float32)
            out.append(-(vx * (after(c) - before(c)) + vel[1] * gy + vel[2] * gz))
        return out

    plane = lambda i: lambda c: order[i][0][c, order[i][1]]
    for i in range(1, 5):
        f0 = rate(plane(i - 1), plane(i), plane(i + 1))
        for c in range(3):
            mid[c, i - 1] = plane(i)(c) + STEP * f0[c]
            if i in (2, 3):
                b_ref[c, one(i - 2)] = f0[c] * (-0.5 * STEP)
    for i in (1, 2):
        f1 = rate(lambda c: mid[c, i - 1], lambda c: mid[c, i], lambda c: mid[c, i + 1])
        for c in range(3):
            at = one(i - 1)
            u1 = mid[c, i]
            a_ref[c, at] = u1 + STEP * f1[c]
            b_ref[c, at] = b_ref[c, at] + (0.5 * STEP) * f1[c] + first * u1


def evaluate(flags, near, own, far, wall, span, flow):
    shape = jax.ShapeDtypeStruct(own.shape, own.dtype)
    vmem = pl.BlockSpec(memory_space=pltpu.VMEM)
    parts, planes, ys, zs = own.shape
    return pl.pallas_call(
        advance,
        out_shape=(shape, shape),
        in_specs=[pl.BlockSpec(memory_space=pltpu.SMEM)] + [vmem] * 6,
        out_specs=(vmem, vmem),
        scratch_shapes=[pltpu.VMEM((parts, planes + 2, ys, zs), jnp.float32)],
        cost_estimate=pl.CostEstimate(flops=6 * 6 * 2 * ys * ys * zs, bytes_accessed=5 * own.size * 4, transcendentals=0),
        name="advance",
    )(flags, near, own, far, wall, span, flow)


def local(ways, start_states, wall_normal, spanwise, base_flow):
    home = start_states[0]
    slice_at, slab_at = lax.axis_index("tm"), lax.axis_index("space")
    core, chip = slice_at % 2, slab_at % 2
    mover = core != chip
    first = (slice_at // 2 == 0) & (chip == 0)
    flags = jnp.stack([core, first.astype(core.dtype)]).astype(jnp.int32)
    flow = jnp.broadcast_to(base_flow[:, :, None], base_flow.shape + home.shape[-1:])
    send = lambda what, way: lax.ppermute(what, AXES, ways[way])
    step = functools.partial(evaluate, flags, wall=wall_normal, span=spanwise, flow=flow)

    swapped = send(home, "swap")
    far_in = send(home, "far_in")
    near_in = send(home, "near_in")
    far_out = send(swapped, "far_out")
    near_out = send(swapped, "near_out")
    a_move, b_move = step(near_in, swapped, far_in)
    back = send(b_move, "swap")
    next_move = send(a_move, "next_move")
    a_stay, b_stay = step(near_out, home, far_out)
    next_stay = send(a_stay, "next_stay")
    return (jnp.where(mover, back, b_stay) + (next_move + next_stay))[None]


def solution(mesh):
    placed = (P("tm", None, "space", None, None), P(), P(), P())
    ways = routes(mesh.shape["tm"], mesh.shape["space"])
    return jax.shard_map(
        functools.partial(local, ways),
        mesh=mesh,
        in_specs=placed,
        out_specs=P("tm", None, "space", None, None),
        check_vma=False,
    )
```

time: 137 us -> 84.4 us (0.62); the launches traced: 135 us -> 84.1 us
  waiting for transfers between devices: 103 us -> 43 us
  Pallas kernels: 0 us -> 14.1 us
  matrix products: 6.41 us -> 0 us
  local copies, waits for them, and re-layouts: 4.75 us -> 2.86 us
  other arithmetic: 2.16 us -> 4.04 us
  starting transfers between devices: 18.3 us -> 20 us
    ppermute x7 -> x8, waiting for transfers between devices: 103 us -> 43 us  [local(): send = lambda what, way: lax.ppermute(what, AXES, ways[way])]
    pallas_call x0 -> x2, Pallas kernels: none -> 14.1 us  [evaluate(): pl.pallas_call(advance, out_shape=(shape, shape), in_specs=[pl.BlockSpec(...]
    dot_general x6 -> x0, matrix products: 6.41 us -> none  [the longest x3 5.16 us: tendency(): jnp.einsum('yk,cxkz->cxyz', wall_normal, rounded, preferred_element_type=...]
    broadcast_in_dim x0 -> x1, other arithmetic: none -> 3.43 us  [local(): return (jnp.where(mover, back, b_stay) + (next_move + next_stay))[None]]
    add x2 -> x0, other arithmetic: 1.78 us -> none  [tendency(): velocity = base_flow[:, None, :, None] + inner]
    ppermute x7 -> x8, starting transfers between devices: 18.3 us -> 20 us  [local(): send = lambda what, way: lax.ppermute(what, AXES, ways[way])]
    unnamed x11 -> x4, local copies, waits for them, and re-layouts: 2.68 us -> 1.13 us
  transfers between devices with their start and end apart: 7 -> 8, of which waited for: 5 -> 4; matrix products, arithmetic and copies ran while one was open for 3% -> 3% of each run, Pallas kernels for 0% -> 17%
where the time goes in v1:
time: 84.4 us; the launch traced here: 84.1 us
  waiting for transfers between devices  43 us (51%)
  starting transfers between devices  20 us (24%)
  Pallas kernels  14.1 us (17%)
  other arithmetic  4.04 us (5%)
  local copies, waits for them, and re-layouts  2.86 us (3%)
    ppermute x8, waiting for transfers between devices, local(): send = lambda what, way: lax.ppermute(what, AXES, ways[way])  43 us
    ppermute x8, starting transfers between devices, local(): send = lambda what, way: lax.ppermute(what, AXES, ways[way])  20 us
    pallas_call x2, Pallas kernels, evaluate(): pl.pallas_call(advance, out_shape=(shape, shape), in_specs=[pl.BlockSpec(...  14.1 us
    broadcast_in_dim x1, other arithmetic, local(): return (jnp.where(mover, back, b_stay) + (next_move + next_stay))[None]  3.43 us
    broadcast_in_dim x1, local copies, waits for them, and re-layouts, local(): jnp.broadcast_to(base_flow[:, :, None], base_flow.shape + home.shape[-1:])  1.73 us
  transfers between devices with their start and end apart: 8, of which 4 were waited for; matrix products, arithmetic and copies ran while one was open for 3% of the time, Pallas kernels for 17%

profile of v1, /device:TPU:113, one launch (start us, length us, event | category | flops | bytes accessed | tf_op | source)
XLA Modules:
  0.0 84.1 jit_solution(257895336905617906)
XLA Ops:
  0.0 3.5 %collective-permute-start.1 = (f32[3,2,256,256]{3,2,1,0:T(8,128)}, f32[3,2,256,256]{3,2,1,0:T(8,128)S(1)}, u32[]{:S(2)}, u32[]{:S(2)}) collective-permute-start(f32[3,2,256,256]{3,2,1,0:T(8,128)} %bitcast.5), channel_id=1, source_target_pairs={{8,1},{1,8},{10,3},{3,10},{12,5},{5,12},{14,7},{7,14},{24,17},{17,... | collective-permute-start | bytes 4718600 | tf_op jit(solution)/shard_map/ppermute | solution.py:91
  3.5 1.3 %collective-permute-start = (f32[3,2,256,256]{3,2,1,0:T(8,128)}, f32[3,2,256,256]{3,2,1,0:T(8,128)}, u32[]{:S(2)}, u32[]{:S(2)}) collective-permute-start(f32[3,2,256,256]{3,2,1,0:T(8,128)} %bitcast.6), channel_id=1, source_target_pairs={{0,8},{9,1},{2,10},{11,3},{4,12},{13,5},{6,14},{15,7},{16,24},{25,... | collective-permute-start | bytes 4718600 | tf_op jit(solution)/shard_map/ppermute | solution.py:91
  4.8 1.3 %collective-permute-start.2 = (f32[3,2,256,256]{3,2,1,0:T(8,128)}, f32[3,2,256,256]{3,2,1,0:T(8,128)}, u32[]{:S(2)}, u32[]{:S(2)}) collective-permute-start(f32[3,2,256,256]{3,2,1,0:T(8,128)} %bitcast.7), channel_id=1, source_target_pairs={{2,8},{15,1},{4,10},{9,3},{6,12},{11,5},{0,14},{13,7},{18,24},{31,... | collective-permute-start | bytes 4718600 | tf_op jit(solution)/shard_map/ppermute | solution.py:91
  6.1 15.9 %collective-permute-done.1.own = f32[3,2,256,256]{3,2,1,0:T(8,128)S(1)} collective-permute-done((f32[3,2,256,256]{3,2,1,0:T(8,128)}, f32[3,2,256,256]{3,2,1,0:T(8,128)S(1)}, u32[]{:S(2)}, u32[]{:S(2)}) %collective-permute-start.1) | collective-permute-done | bytes 1572896 | tf_op jit(solution)/shard_map/ppermute | solution.py:91
  21.9 0.0 copy-start
  21.9 1.4 %collective-permute-start.4 = (f32[3,2,256,256]{3,2,1,0:T(8,128)S(1)}, f32[3,2,256,256]{3,2,1,0:T(8,128)S(1)}, u32[]{:S(2)}, u32[]{:S(2)}) collective-permute-start(f32[3,2,256,256]{3,2,1,0:T(8,128)S(1)} %collective-permute-done.1.own), channel_id=1, source_target_pairs={{8,0},{1,9},{10,2},{3,11},{12,4},{5,13},{14,6},{7,15},{24,16},{17,... | collective-permute-start | bytes 4718600 | tf_op jit(solution)/shard_map/ppermute | solution.py:91
  23.3 2.5 %collective-permute-start.5 = (f32[3,2,256,256]{3,2,1,0:T(8,128)S(1)}, f32[3,2,256,256]{3,2,1,0:T(8,128)}, u32[]{:S(2)}, u32[]{:S(2)}) collective-permute-start(f32[3,2,256,256]{3,2,1,0:T(8,128)S(1)} %collective-permute-done.1.own), channel_id=1, source_target_pairs={{8,2},{1,15},{10,4},{3,9},{12,6},{5,11},{14,0},{7,13},{24,18},{17,... | collective-permute-start | bytes 4718600 | tf_op jit(solution)/shard_map/ppermute | solution.py:91
  25.8 0.6 pad_add_fusion.flags
  26.4 0.0 collective-permute-done.near
  26.4 1.5 %collective-permute-done.2.far = f32[3,2,256,256]{3,2,1,0:T(8,128)} collective-permute-done((f32[3,2,256,256]{3,2,1,0:T(8,128)}, f32[3,2,256,256]{3,2,1,0:T(8,128)}, u32[]{:S(2)}, u32[]{:S(2)}) %collective-permute-start.2) | collective-permute-done | bytes 1572896 | tf_op jit(solution)/shard_map/ppermute | solution.py:91
  27.8 1.7 %broadcast_in_dim.4.flow = f32[3,256,256]{2,1,0:T(8,128)} broadcast(f32[3,256]{1,0:T(4,128)} %param.7), dimensions={0,1} | broadcast | bytes 789504 | tf_op jit(solution)/shard_map/broadcast_in_dim | solution.py:90
  29.6 0.0 copy-done
  29.6 7.0 %advance.2 = (f32[3,2,256,256]{3,2,1,0:T(8,128)}, f32[3,2,256,256]{3,2,1,0:T(8,128)}) custom-call(s32[2]{0:T(128)} %pad_add_fusion.flags, f32[3,2,256,256]{3,2,1,0:T(8,128)} %collective-permute-done.near, f32[3,2,256,256]{3,2,1,0:T(8,128)} %copy-done, f32[3,2,256,256]{3,2,1,0:T(8,128)} %collective-permute-done.2.far, bf16[256,256]{1,0:T(8,128)(2,1)} %wall.3, ...), custom_call_target="tpu_custom_call" | custom-call | flops 1207959552 | bytes 7864320 | tf_op jit(solution)/shard_map/advance/pallas_call | solution.py:72
  36.5 2.5 %collective-permute-start.6 = (f32[3,2,256,256]{3,2,1,0:T(8,128)}, f32[3,2,256,256]{3,2,1,0:T(8,128)}, u32[]{:S(2)}, u32[]{:S(2)}) collective-permute-start(f32[3,2,256,256]{3,2,1,0:T(8,128)} %get-tuple-element.11), channel_id=1, source_target_pairs={{8,9},{1,16},{10,11},{3,18},{12,13},{5,20},{14,15},{7,22},{24,25},... | collective-permute-start | bytes 4718600 | tf_op jit(solution)/shard_map/ppermute | solution.py:91
  39.0 6.4 %collective-permute-start.3 = (f32[3,2,256,256]{3,2,1,0:T(8,128)}, f32[3,2,256,256]{3,2,1,0:T(8,128)}, u32[]{:S(2)}, u32[]{:S(2)}) collective-permute-start(f32[3,2,256,256]{3,2,1,0:T(8,128)} %get-tuple-element.9), channel_id=1, source_target_pairs={{8,1},{1,8},{10,3},{3,10},{12,5},{5,12},{14,7},{7,14},{24,17},{17,... | collective-permute-start | bytes 4718600 | tf_op jit(solution)/shard_map/ppermute | solution.py:91
  45.4 0.0 collective-permute-done.4.near
  45.4 0.0 copy-start.1
  45.5 0.0 collective-permute-done.5.far
  45.5 1.1 %copy-done.1 = f32[3,2,256,256]{3,2,1,0:T(8,128)} copy-done((f32[3,2,256,256]{3,2,1,0:T(8,128)}, f32[3,2,256,256]{3,2,1,0:T(8,128)S(1)}, u32[]{:S(2)}) %copy-start.1) | copy-done | bytes 1572888
  46.6 7.1 %advance.3 = (f32[3,2,256,256]{3,2,1,0:T(8,128)}, f32[3,2,256,256]{3,2,1,0:T(8,128)}) custom-call(s32[2]{0:T(128)} %pad_add_fusion.flags, f32[3,2,256,256]{3,2,1,0:T(8,128)} %copy-done.1, f32[3,2,256,256]{3,2,1,0:T(8,128)} %bitcast.8, f32[3,2,256,256]{3,2,1,0:T(8,128)} %collective-permute-done.5.far, bf16[256,256]{1,0:T(8,128)(2,1)} %wall.3, ...), custom_call_target="tpu_custom_call" | custom-call | flops 1207959552 | bytes 7864320 | tf_op jit(solution)/shard_map/advance/pallas_call | solution.py:72
  53.7 1.3 %collective-permute-start.7 = (f32[3,2,256,256]{3,2,1,0:T(8,128)}, f32[3,2,256,256]{3,2,1,0:T(8,128)S(1)}, u32[]{:S(2)}, u32[]{:S(2)}) collective-permute-start(f32[3,2,256,256]{3,2,1,0:T(8,128)} %get-tuple-element.12), channel_id=1, source_target_pairs={{0,8},{9,17},{2,10},{11,19},{4,12},{13,21},{6,14},{15,23},{16,24},... | collective-permute-start | bytes 4718600 | tf_op jit(solution)/shard_map/ppermute | solution.py:91
  55.0 0.5 collective-permute-done.6
  55.5 25.2 %collective-permute-done.3 = f32[3,2,256,256]{3,2,1,0:T(8,128)} collective-permute-done((f32[3,2,256,256]{3,2,1,0:T(8,128)}, f32[3,2,256,256]{3,2,1,0:T(8,128)}, u32[]{:S(2)}, u32[]{:S(2)}) %collective-permute-start.3) | collective-permute-done | bytes 1572896 | tf_op jit(solution)/shard_map/ppermute | solution.py:91
  80.7 0.0 collective-permute-done.7
  80.7 3.4 %add_bitcast_fusion = f32[1,3,2,256,256]{4,3,2,1,0:T(8,128)} fusion(f32[3,2,256,256]{3,2,1,0:T(8,128)} %collective-permute-done.6, f32[3,2,256,256]{3,2,1,0:T(8,128)S(1)} %collective-permute-done.7, f32[3,2,256,256]{3,2,1,0:T(8,128)} %collective-permute-done.3, f32[3,2,256,256]{3,2,1,0:T(8,128)} %get-tuple-element.10, pred[]{:T(512)S(6)} %ne.21), kind=kLoop, calls=%fused_computation | loop fusion | flops 1179648 | bytes 7864321 | tf_op jit(solution)/shard_map/broadcast_in_dim | solution.py:104
Async XLA Ops:
  0.0 21.9 %collective-permute-start.1 = (f32[3,2,256,256]{3,2,1,0:T(8,128)}, f32[3,2,256,256]{3,2,1,0:T(8,128)S(1)}, u32[]{:S(2)}, u32[]{:S(2)}) collective-permute-start(f32[3,2,256,256]{3,2,1,0:T(8,128)} %bitcast.5), channel_id=1, source_target_pairs={{8,1},{1,8},{10,3},{3,10},{12,5},{5,12},{14,7},{7,14},{24,17},{17,... | collective-permute-start | bytes 4718600 | tf_op jit(solution)/shard_map/ppermute | solution.py:91
  3.5 22.9 %collective-permute-start = (f32[3,2,256,256]{3,2,1,0:T(8,128)}, f32[3,2,256,256]{3,2,1,0:T(8,128)}, u32[]{:S(2)}, u32[]{:S(2)}) collective-permute-start(f32[3,2,256,256]{3,2,1,0:T(8,128)} %bitcast.6), channel_id=1, source_target_pairs={{0,8},{9,1},{2,10},{11,3},{4,12},{13,5},{6,14},{15,7},{16,24},{25,... | collective-permute-start | bytes 4718600 | tf_op jit(solution)/shard_map/ppermute | solution.py:91
  4.8 23.1 %collective-permute-start.2 = (f32[3,2,256,256]{3,2,1,0:T(8,128)}, f32[3,2,256,256]{3,2,1,0:T(8,128)}, u32[]{:S(2)}, u32[]{:S(2)}) collective-permute-start(f32[3,2,256,256]{3,2,1,0:T(8,128)} %bitcast.7), channel_id=1, source_target_pairs={{2,8},{15,1},{4,10},{9,3},{6,12},{11,5},{0,14},{13,7},{18,24},{31,... | collective-permute-start | bytes 4718600 | tf_op jit(solution)/shard_map/ppermute | solution.py:91
  21.9 7.6 %copy-start = (f32[3,2,256,256]{3,2,1,0:T(8,128)}, f32[3,2,256,256]{3,2,1,0:T(8,128)S(1)}, u32[]{:S(2)}) copy-start(f32[3,2,256,256]{3,2,1,0:T(8,128)S(1)} %collective-permute-done.1.own) | copy-start | bytes 4718596
  21.9 23.5 %collective-permute-start.4 = (f32[3,2,256,256]{3,2,1,0:T(8,128)S(1)}, f32[3,2,256,256]{3,2,1,0:T(8,128)S(1)}, u32[]{:S(2)}, u32[]{:S(2)}) collective-permute-start(f32[3,2,256,256]{3,2,1,0:T(8,128)S(1)} %collective-permute-done.1.own), channel_id=1, source_target_pairs={{8,0},{1,9},{10,2},{3,11},{12,4},{5,13},{14,6},{7,15},{24,16},{17,... | collective-permute-start | bytes 4718600 | tf_op jit(solution)/shard_map/ppermute | solution.py:91
  23.3 22.1 %collective-permute-start.5 = (f32[3,2,256,256]{3,2,1,0:T(8,128)S(1)}, f32[3,2,256,256]{3,2,1,0:T(8,128)}, u32[]{:S(2)}, u32[]{:S(2)}) collective-permute-start(f32[3,2,256,256]{3,2,1,0:T(8,128)S(1)} %collective-permute-done.1.own), channel_id=1, source_target_pairs={{8,2},{1,15},{10,4},{3,9},{12,6},{5,11},{14,0},{7,13},{24,18},{17,... | collective-permute-start | bytes 4718600 | tf_op jit(solution)/shard_map/ppermute | solution.py:91
  36.5 18.9 %collective-permute-start.6 = (f32[3,2,256,256]{3,2,1,0:T(8,128)}, f32[3,2,256,256]{3,2,1,0:T(8,128)}, u32[]{:S(2)}, u32[]{:S(2)}) collective-permute-start(f32[3,2,256,256]{3,2,1,0:T(8,128)} %get-tuple-element.11), channel_id=1, source_target_pairs={{8,9},{1,16},{10,11},{3,18},{12,13},{5,20},{14,15},{7,22},{24,25},... | collective-permute-start | bytes 4718600 | tf_op jit(solution)/shard_map/ppermute | solution.py:91
  39.0 41.7 %collective-permute-start.3 = (f32[3,2,256,256]{3,2,1,0:T(8,128)}, f32[3,2,256,256]{3,2,1,0:T(8,128)}, u32[]{:S(2)}, u32[]{:S(2)}) collective-permute-start(f32[3,2,256,256]{3,2,1,0:T(8,128)} %get-tuple-element.9), channel_id=1, source_target_pairs={{8,1},{1,8},{10,3},{3,10},{12,5},{5,12},{14,7},{7,14},{24,17},{17,... | collective-permute-start | bytes 4718600 | tf_op jit(solution)/shard_map/ppermute | solution.py:91
  45.4 1.1 %copy-start.1 = (f32[3,2,256,256]{3,2,1,0:T(8,128)}, f32[3,2,256,256]{3,2,1,0:T(8,128)S(1)}, u32[]{:S(2)}) copy-start(f32[3,2,256,256]{3,2,1,0:T(8,128)S(1)} %collective-permute-done.4.near) | copy-start | bytes 4718596
  53.7 27.0 %collective-permute-start.7 = (f32[3,2,256,256]{3,2,1,0:T(8,128)}, f32[3,2,256,256]{3,2,1,0:T(8,128)S(1)}, u32[]{:S(2)}, u32[]{:S(2)}) collective-permute-start(f32[3,2,256,256]{3,2,1,0:T(8,128)} %get-tuple-element.12), channel_id=1, source_target_pairs={{0,8},{9,17},{2,10},{11,19},{4,12},{13,21},{6,14},{15,23},{16,24},... | collective-permute-start | bytes 4718600 | tf_op jit(solution)/shard_map/ppermute | solution.py:91

commit v2 on v1

v2 whole, which is shorter than its diff:
```python
import functools

import jax
import jax.numpy as jnp
from jax import lax
from jax.experimental import pallas as pl
from jax.experimental.pallas import tpu as pltpu
from jax.sharding import PartitionSpec as P


AXES = ("tm", "space")
STEP = 0.2
EARLY = 2


def routes(slices, slabs):
    at = lambda s, p: s * slabs + p % slabs
    cells = [(k, x, l) for k in range(slices // 2) for x in range(slabs // 2) for l in range(2)]
    side = lambda l: 1 - 2 * l
    stay = lambda k, x, l: at(2 * k + l, 2 * x + l)
    move = lambda k, x, l: at(2 * k + 1 - l, 2 * x + l)
    return {
        "swap": [(move(k, x, l), move(k, x, 1 - l)) for k, x, l in cells],
        "near_in": [(stay(k, x, l), move(k, x, l)) for k, x, l in cells],
        "far_in": [(stay(k, x + side(l), l), move(k, x, l)) for k, x, l in cells],
        "near_out": [(move(k, x, l), stay(k, x, l)) for k, x, l in cells],
        "far_out": [(move(k, x, l), stay(k, x + side(l), l)) for k, x, l in cells],
        "next_move": [
            (move(k, x, l), at(2 * k + l + 1, 2 * x + 1 - l)) for k, x, l in cells if 2 * k + l + 1 < slices
        ],
        "next_stay": [(stay(k, x, l), at(2 * k + l + 1, 2 * x + l)) for k, x, l in cells if 2 * k + l + 1 < slices],
    }


def advance(sizes, *refs):
    pieces, refs = refs[: sum(map(len, sizes))], refs[sum(map(len, sizes)) :]
    wall, span, base, a_early, a_late, b_out, mid, a_mid, b_mid, flow, out_sems = refs
    slice_at, slab_at = lax.axis_index(AXES[0]), lax.axis_index(AXES[1])
    low = slice_at % 2
    leading = (slice_at < 2) & (slab_at % 2 == 0)
    half = jnp.where(low == 1, 0.5, -0.5).astype(jnp.float32)
    slot = lambda i: jnp.where(low == 1, i % 2, 1 - i % 2)

    plane = []
    for i in range(6):
        first_piece = sum(len(sizes[k]) for k in range(i // 2))
        plane.append(
            [
                (pieces[first_piece + n], c)
                for n, size in enumerate(sizes[i // 2])
                for c in range(size)
            ]
        )

    def load(i):
        return lambda c: plane[i][c][0][plane[i][c][1], slot(i)]

    for c in range(3):
        rows = jnp.broadcast_to(base[c : c + 1], (8, base.shape[1]))
        flow[c] = jnp.broadcast_to(rows.T[:, :1], flow.shape[1:])

    def slope(before, here, after):
        fields = [here(c) for c in range(3)]
        vx, vy, vz = [jnp.concatenate([flow[c]] * 2, axis=1) + fields[c] for c in range(3)]
        vx = vx * half
        for c in range(3):
            rounded = fields[c].astype(jnp.bfloat16)
            gy = jnp.dot(wall[...], rounded, preferred_element_type=jnp.float32)
            gz = jnp.dot(rounded, span[...], preferred_element_type=jnp.float32)
            yield fields[c], vx * (after(c) - before(c)) + vy * gy + vz * gz

    def inner(i):
        for c, (u0, g0) in enumerate(slope(load(i - 1), load(i), load(i + 1))):
            mid[c, i - 1] = u0 - STEP * g0
            if i in (2, 3):
                b_mid[c, i - 2] = g0 * (0.5 * STEP)

    def outer(i):
        for c, (u1, g1) in enumerate(slope(*[lambda c, k=k: mid[c, k] for k in (i - 2, i - 1, i)])):
            a_mid[c, i - 2] = u1 - STEP * g1
            b_mid[c, i - 2] = b_mid[c, i - 2] - (0.5 * STEP) * g1

        @pl.when(leading)
        def _():
            b_mid[:, i - 2] = b_mid[:, i - 2] + mid[:, i - 1]

        place = i - 2, slot(i)
        sends = [
            pltpu.make_async_copy(value.at[:, place[0]], out.at[:, place[1]], out_sems.at[n, i - 2])
            for n, (value, out) in enumerate(
                ((b_mid, b_out), (a_mid.at[:EARLY], a_early), (a_mid.at[EARLY:], a_late))
            )
        ]
        for send in sends:
            send.start()
        return sends

    inner(1)
    inner(2)
    inner(3)
    sends = outer(2)
    inner(4)
    sends += outer(3)
    for send in sends:
        send.wait()


def evaluate(slabs, wall, span, base):
    sizes = [[piece.shape[0] for piece in slab] for slab in slabs]
    pieces = [piece for slab in slabs for piece in slab]
    planes, ys, zs = pieces[0].shape[1:]
    shape = lambda n: jax.ShapeDtypeStruct((n, planes, ys, zs), jnp.float32)
    vmem = pl.BlockSpec(memory_space=pltpu.VMEM)
    any_space = pl.BlockSpec(memory_space=pl.ANY)
    block = lambda n: pltpu.VMEM((3, n, ys, zs), jnp.float32)
    return pl.pallas_call(
        functools.partial(advance, sizes),
        out_shape=(shape(EARLY), shape(3 - EARLY), shape(3)),
        in_specs=[vmem] * (len(pieces) + 3),
        out_specs=(any_space,) * 3,
        scratch_shapes=[
            block(4),
            block(2),
            block(2),
            pltpu.VMEM((3, ys, zs // 2), jnp.float32),
            pltpu.SemaphoreType.DMA((3, 2)),
        ],
        compiler_params=pltpu.CompilerParams(vmem_limit_bytes=12 * 2**20),
        cost_estimate=pl.CostEstimate(flops=36 * 2 * ys * ys * zs, bytes_accessed=30 * ys * zs * 4, transcendentals=0),
        name="advance",
    )(*pieces, wall, span, base)


def local(ways, start_states, wall_normal, spanwise, base_flow):
    home = start_states[0]
    mover = lax.axis_index("tm") % 2 != lax.axis_index("space") % 2
    step = functools.partial(evaluate, wall=wall_normal, span=spanwise, base=base_flow)

    def send(what, way):
        return lax.ppermute(what, AXES, ways[way])

    far_in = send(home, "far_in")
    own_early = send(home[:EARLY], "swap")
    own_late = send(home[EARLY:], "swap")
    near_in = send(home, "near_in")
    far_early = send(own_early, "far_out")
    near_early = send(own_early, "near_out")
    move_early, move_late, b_move = step([[near_in], [own_early, own_late], [far_in]])
    back = send(b_move, "swap")
    far_late = send(own_late, "far_out")
    move_early = send(move_early, "next_move")
    move_late = send(move_late, "next_move")
    near_late = send(own_late, "near_out")
    stay_early, stay_late, b_stay = step([[near_early, near_late], [home], [far_early, far_late]])
    stay_early = send(stay_early, "next_stay")
    stay_late = send(stay_late, "next_stay")
    result = jnp.where(mover, back, b_stay)
    result = result.at[:EARLY].add(jnp.where(mover, stay_early, move_early))
    result = result.at[EARLY:].add(jnp.where(mover, stay_late, move_late))
    return result[None]


def solution(mesh):
    placed = (P("tm", None, "space", None, None), P(), P(), P())
    ways = routes(mesh.shape["tm"], mesh.shape["space"])
    return jax.shard_map(
        functools.partial(local, ways),
        mesh=mesh,
        in_specs=placed,
        out_specs=P("tm", None, "space", None, None),
        check_vma=False,
    )
```

time: 84.4 us -> 79.8 us (0.945)
  the two profiles are of different devices: /device:TPU:113 before, /device:TPU:136 now
where the time goes in v2:
time: 79.8 us; the launch traced here: 79.4 us
  starting transfers between devices  32.2 us (40%)
  waiting for transfers between devices  30.9 us (39%)
  Pallas kernels  8.58 us (11%)
  other arithmetic  4.15 us (5%)
  local copies, waits for them, and re-layouts  3.31 us (4%)
    ppermute x13, starting transfers between devices, send(): return lax.ppermute(what, AXES, ways[way])  32.2 us
    ppermute x13, waiting for transfers between devices, send(): return lax.ppermute(what, AXES, ways[way])  30.9 us
    pallas_call x2, Pallas kernels, evaluate(): pl.pallas_call(functools.partial(advance, sizes), out_shape=(shape(EARLY)...  8.58 us
    unnamed x13, local copies, waits for them, and re-layouts  1.97 us
    scatter-add x1, other arithmetic, local(): result = result.at[:EARLY].add(jnp.where(mover, stay_early, move_early))  1.63 us
    select_n x1, other arithmetic, local(): result = jnp.where(mover, back, b_stay)  1.62 us
  transfers between devices with their start and end apart: 13, of which 6 were waited for; matrix products, arithmetic and copies ran while one was open for 7% of the time, Pallas kernels for 11%

profile of v2, /device:TPU:136, one launch (start us, length us, event | category | flops | bytes accessed | tf_op | source)
XLA Modules:
  0.0 79.4 jit_solution(5000550585495811948)
XLA Ops:
  0.0 1.4 %collective-permute-start = (f32[3,2,256,256]{3,2,1,0:T(8,128)}, f32[3,2,256,256]{3,2,1,0:T(8,128)S(1)}, u32[]{:S(2)}, u32[]{:S(2)}) collective-permute-start(f32[3,2,256,256]{3,2,1,0:T(8,128)} %bitcast.10), channel_id=1, source_target_pairs={{0,8},{9,1},{2,10},{11,3},{4,12},{13,5},{6,14},{15,7},{16,24},{25,... | collective-permute-start | bytes 4718600 | tf_op jit(solution)/shard_map/ppermute | solution.py:140
  1.5 1.3 %collective-permute-start.3 = (f32[3,2,256,256]{3,2,1,0:T(8,128)}, f32[3,2,256,256]{3,2,1,0:T(8,128)S(1)}, u32[]{:S(2)}, u32[]{:S(2)}) collective-permute-start(f32[3,2,256,256]{3,2,1,0:T(8,128)} %bitcast.11), channel_id=1, source_target_pairs={{2,8},{15,1},{4,10},{9,3},{6,12},{11,5},{0,14},{13,7},{18,24},{31,... | collective-permute-start | bytes 4718600 | tf_op jit(solution)/shard_map/ppermute | solution.py:140
  2.8 1.3 %slice_bitcast_fusion = f32[2,2,256,256]{3,2,1,0:T(8,128)S(1)} fusion(f32[1,3,2,256,256]{4,3,2,1,0:T(8,128)} %param.8), kind=kLoop, calls=%fused_computation.2 | loop fusion | bytes 2097152 | tf_op jit(solution)/shard_map/slice | solution.py:143
  4.1 1.9 %collective-permute-start.1 = (f32[2,2,256,256]{3,2,1,0:T(8,128)S(1)}, f32[2,2,256,256]{3,2,1,0:T(8,128)S(1)}, u32[]{:S(2)}, u32[]{:S(2)}) collective-permute-start(f32[2,2,256,256]{3,2,1,0:T(8,128)S(1)} %slice_bitcast_fusion), channel_id=1, source_target_pairs={{8,1},{1,8},{10,3},{3,10},{12,5},{5,12},{14,7},{7,14},{24,17},{17,... | collective-permute-start | bytes 3145736 | tf_op jit(solution)/shard_map/ppermute | solution.py:140
  6.0 3.6 %collective-permute-start.2 = (f32[1,2,256,256]{3,2,1,0:T(8,128)S(1)}, f32[1,2,256,256]{3,2,1,0:T(8,128)S(1)}, u32[]{:S(2)}, u32[]{:S(2)}) collective-permute-start(f32[1,2,256,256]{3,2,1,0:T(8,128)S(1)} %slice_bitcast_fusion.1), channel_id=1, source_target_pairs={{8,1},{1,8},{10,3},{3,10},{12,5},{5,12},{14,7},{7,14},{24,17},{17,... | collective-permute-start | bytes 1572872 | tf_op jit(solution)/shard_map/ppermute | solution.py:140
  9.7 10.5 %collective-permute-done.1.refs_1_ = f32[2,2,256,256]{3,2,1,0:T(8,128)S(1)} collective-permute-done((f32[2,2,256,256]{3,2,1,0:T(8,128)S(1)}, f32[2,2,256,256]{3,2,1,0:T(8,128)S(1)}, u32[]{:S(2)}, u32[]{:S(2)}) %collective-permute-start.1) | collective-permute-done | bytes 1048608 | tf_op jit(solution)/shard_map/ppermute | solution.py:140
  20.2 1.3 %collective-permute-start.5 = (f32[2,2,256,256]{3,2,1,0:T(8,128)S(1)}, f32[2,2,256,256]{3,2,1,0:T(8,128)S(1)}, u32[]{:S(2)}, u32[]{:S(2)}) collective-permute-start(f32[2,2,256,256]{3,2,1,0:T(8,128)S(1)} %collective-permute-done.1.refs_1_), channel_id=1, source_target_pairs={{8,0},{1,9},{10,2},{3,11},{12,4},{5,13},{14,6},{7,15},{24,16},{17,... | collective-permute-start | bytes 3145736 | tf_op jit(solution)/shard_map/ppermute | solution.py:140
  21.5 1.4 %collective-permute-start.7 = (f32[2,2,256,256]{3,2,1,0:T(8,128)S(1)}, f32[2,2,256,256]{3,2,1,0:T(8,128)S(1)}, u32[]{:S(2)}, u32[]{:S(2)}) collective-permute-start(f32[2,2,256,256]{3,2,1,0:T(8,128)S(1)} %collective-permute-done.1.refs_1_), channel_id=1, source_target_pairs={{8,2},{1,15},{10,4},{3,9},{12,6},{5,11},{14,0},{7,13},{24,18},{17,... | collective-permute-start | bytes 3145736 | tf_op jit(solution)/shard_map/ppermute | solution.py:140
  22.9 2.9 %collective-permute-done.2.refs_2_ = f32[1,2,256,256]{3,2,1,0:T(8,128)S(1)} collective-permute-done((f32[1,2,256,256]{3,2,1,0:T(8,128)S(1)}, f32[1,2,256,256]{3,2,1,0:T(8,128)S(1)}, u32[]{:S(2)}, u32[]{:S(2)}) %collective-permute-start.2) | collective-permute-done | bytes 524320 | tf_op jit(solution)/shard_map/ppermute | solution.py:140
  25.8 0.0 collective-permute-done.refs_0_
  25.8 0.0 collective-permute-done.3.refs_3_
  25.8 4.4 %advance.2 = (f32[2,2,256,256]{3,2,1,0:T(8,128)}, f32[1,2,256,256]{3,2,1,0:T(8,128)S(1)}, f32[3,2,256,256]{3,2,1,0:T(8,128)S(1)}) custom-call(f32[3,2,256,256]{3,2,1,0:T(8,128)S(1)} %collective-permute-done.refs_0_, f32[2,2,256,256]{3,2,1,0:T(8,128)S(1)} %collective-permute-done.1.refs_1_, f32[1,2,256,256]{3,2,1,0:T(8,128)S(1)} %collective-permute-done.2.refs_2_, ...), custom_call_target="tpu_custom_call" | custom-call | flops 1207959552 | bytes 7864320 | tf_op jit(solution)/shard_map/advance/pallas_call | solution.py:116
  30.2 1.9 %collective-permute-start.4 = (f32[3,2,256,256]{3,2,1,0:T(8,128)S(1)}, f32[3,2,256,256]{3,2,1,0:T(8,128)}, u32[]{:S(2)}, u32[]{:S(2)}) collective-permute-start(f32[3,2,256,256]{3,2,1,0:T(8,128)S(1)} %get-tuple-element.35), channel_id=1, source_target_pairs={{8,1},{1,8},{10,3},{3,10},{12,5},{5,12},{14,7},{7,14},{24,17},{17,... | collective-permute-start | bytes 4718600 | tf_op jit(solution)/shard_map/ppermute | solution.py:140
  32.2 1.3 %collective-permute-start.6 = (f32[1,2,256,256]{3,2,1,0:T(8,128)S(1)}, f32[1,2,256,256]{3,2,1,0:T(8,128)S(1)}, u32[]{:S(2)}, u32[]{:S(2)}) collective-permute-start(f32[1,2,256,256]{3,2,1,0:T(8,128)S(1)} %collective-permute-done.2.refs_2_), channel_id=1, source_target_pairs={{8,0},{1,9},{10,2},{3,11},{12,4},{5,13},{14,6},{7,15},{24,16},{17,... | collective-permute-start | bytes 1572872 | tf_op jit(solution)/shard_map/ppermute | solution.py:140
  33.5 1.3 %collective-permute-start.8 = (f32[1,2,256,256]{3,2,1,0:T(8,128)S(1)}, f32[1,2,256,256]{3,2,1,0:T(8,128)S(1)}, u32[]{:S(2)}, u32[]{:S(2)}) collective-permute-start(f32[1,2,256,256]{3,2,1,0:T(8,128)S(1)} %collective-permute-done.2.refs_2_), channel_id=1, source_target_pairs={{8,2},{1,15},{10,4},{3,9},{12,6},{5,11},{14,0},{7,13},{24,18},{17,... | collective-permute-start | bytes 1572872 | tf_op jit(solution)/shard_map/ppermute | solution.py:140
  34.8 0.2 collective-permute-done.6.refs_1_
  35.0 5.7 %collective-permute-start.10 = (f32[2,2,256,256]{3,2,1,0:T(8,128)}, f32[2,2,256,256]{3,2,1,0:T(8,128)}, u32[]{:S(2)}, u32[]{:S(2)}) collective-permute-start(f32[2,2,256,256]{3,2,1,0:T(8,128)} %get-tuple-element.38), channel_id=1, source_target_pairs={{8,9},{1,16},{10,11},{3,18},{12,13},{5,20},{14,15},{7,22},{24,25},... | collective-permute-start | bytes 3145736 | tf_op jit(solution)/shard_map/ppermute | solution.py:140
  40.7 0.8 collective-permute-done.8.refs_4_
  41.5 0.0 collective-permute-done.5.refs_0_
  41.5 4.2 %advance.3 = (f32[2,2,256,256]{3,2,1,0:T(8,128)}, f32[1,2,256,256]{3,2,1,0:T(8,128)S(1)}, f32[3,2,256,256]{3,2,1,0:T(8,128)S(1)}) custom-call(f32[2,2,256,256]{3,2,1,0:T(8,128)S(1)} %collective-permute-done.5.refs_0_, f32[1,2,256,256]{3,2,1,0:T(8,128)S(1)} %collective-permute-done.6.refs_1_, f32[3,2,256,256]{3,2,1,0:T(8,128)S(1)} %bitcast.12, ...), custom_call_target="tpu_custom_call" | custom-call | flops 1207959552 | bytes 7864320 | tf_op jit(solution)/shard_map/advance/pallas_call | solution.py:116
  45.7 0.8 %copy-done.5 = f32[1,2,256,256]{3,2,1,0:T(8,128)} copy-done((f32[1,2,256,256]{3,2,1,0:T(8,128)}, f32[1,2,256,256]{3,2,1,0:T(8,128)S(1)}, u32[]{:S(2)}) %copy-start.5) | copy-done | bytes 524312
  46.5 1.3 %collective-permute-start.9 = (f32[2,2,256,256]{3,2,1,0:T(8,128)}, f32[2,2,256,256]{3,2,1,0:T(8,128)}, u32[]{:S(2)}, u32[]{:S(2)}) collective-permute-start(f32[2,2,256,256]{3,2,1,0:T(8,128)} %get-tuple-element.37), channel_id=1, source_target_pairs={{0,8},{9,17},{2,10},{11,19},{4,12},{13,21},{6,14},{15,23},{16,24},... | collective-permute-start | bytes 3145736 | tf_op jit(solution)/shard_map/ppermute | solution.py:140
  47.8 8.4 %collective-permute-start.12 = (f32[1,2,256,256]{3,2,1,0:T(8,128)}, f32[1,2,256,256]{3,2,1,0:T(8,128)S(1)}, u32[]{:S(2)}, u32[]{:S(2)}) collective-permute-start(f32[1,2,256,256]{3,2,1,0:T(8,128)} %copy-done.4), channel_id=1, source_target_pairs={{8,9},{1,16},{10,11},{3,18},{12,13},{5,20},{14,15},{7,22},{24,25},... | collective-permute-start | bytes 1572872 | tf_op jit(solution)/shard_map/ppermute | solution.py:140
  56.2 1.3 %collective-permute-start.11 = (f32[1,2,256,256]{3,2,1,0:T(8,128)}, f32[1,2,256,256]{3,2,1,0:T(8,128)S(1)}, u32[]{:S(2)}, u32[]{:S(2)}) collective-permute-start(f32[1,2,256,256]{3,2,1,0:T(8,128)} %copy-done.5), channel_id=1, source_target_pairs={{0,8},{9,17},{2,10},{11,19},{4,12},{13,21},{6,14},{15,23},{16,24},... | collective-permute-start | bytes 1572872 | tf_op jit(solution)/shard_map/ppermute | solution.py:140
  57.5 0.0 collective-permute-done.4
  57.5 1.6 %broadcast_select_fusion = f32[3,2,256,256]{3,2,1,0:T(8,128)S(1)} fusion(f32[3,2,256,256]{3,2,1,0:T(8,128)} %collective-permute-done.4, f32[3,2,256,256]{3,2,1,0:T(8,128)S(1)} %get-tuple-element.36, pred[]{:T(512)S(6)} %ne.15), kind=kLoop, calls=%fused_computation.3 | loop fusion | flops 393216 | bytes 4718593 | tf_op jit(solution)/shard_map/jit(_where)/select_n | solution.py:157
  59.1 0.0 collective-permute-done.10
  59.1 13.9 %collective-permute-done.9 = f32[2,2,256,256]{3,2,1,0:T(8,128)} collective-permute-done((f32[2,2,256,256]{3,2,1,0:T(8,128)}, f32[2,2,256,256]{3,2,1,0:T(8,128)}, u32[]{:S(2)}, u32[]{:S(2)}) %collective-permute-start.9) | collective-permute-done | bytes 1048608 | tf_op jit(solution)/shard_map/ppermute | solution.py:140
  73.0 1.6 %fusion = f32[3,2,256,256]{3,2,1,0:T(8,128)S(1)} fusion(f32[3,2,256,256]{3,2,1,0:T(8,128)S(1)} %broadcast_select_fusion, f32[2,2,256,256]{3,2,1,0:T(8,128)} %collective-permute-done.9, f32[2,2,256,256]{3,2,1,0:T(8,128)} %collective-permute-done.10, pred[]{:T(512)S(6)} %ne.15), kind=kLoop, calls=%fused_computation.1 | loop fusion | flops 524288 | bytes 4194305 | tf_op jit(solution)/shard_map/scatter-add | solution.py:158
  74.6 1.1 %copy.6 = f32[1,3,2,256,256]{4,3,2,1,0:T(8,128)} copy(f32[1,3,2,256,256]{4,3,2,1,0:T(8,128)S(1)} %bitcast.13) | data formatting | bytes 3145728
  75.8 2.7 %collective-permute-done.11 = f32[1,2,256,256]{3,2,1,0:T(8,128)S(1)} collective-permute-done((f32[1,2,256,256]{3,2,1,0:T(8,128)}, f32[1,2,256,256]{3,2,1,0:T(8,128)S(1)}, u32[]{:S(2)}, u32[]{:S(2)}) %collective-permute-start.11) | collective-permute-done | bytes 524320 | tf_op jit(solution)/shard_map/ppermute | solution.py:140
  78.5 0.9 %fusion.2 = f32[1,3,2,256,256]{4,3,2,1,0:T(8,128)} fusion(f32[1,3,2,256,256]{4,3,2,1,0:T(8,128)} %copy.6, f32[3,2,256,256]{3,2,1,0:T(8,128)S(1)} %fusion, f32[1,2,256,256]{3,2,1,0:T(8,128)S(1)} %collective-permute-done.11, f32[1,2,256,256]{3,2,1,0:T(8,128)S(1)} %collective-permute-done.12, pred[]{:T(512)S(6)} %ne.15), kind=kLoop, calls=%fused_computation.6 | loop fusion | flops 262144 | bytes 2097153 | tf_op jit(solution)/shard_map/scatter-add | solution.py:159
  (14 shorter events, 0.1 us)
Async XLA Ops:
  0.0 6.0 %copy-start = (f32[1,3,2,256,256]{4,3,2,1,0:T(8,128)S(1)}, f32[1,3,2,256,256]{4,3,2,1,0:T(8,128)}, u32[]{:S(2)}) copy-start(f32[1,3,2,256,256]{4,3,2,1,0:T(8,128)} %param.8) | copy-start | bytes 4718596
  0.0 25.8 %copy-start.1 = (bf16[256,256]{1,0:T(8,128)(2,1)S(1)}, bf16[256,256]{1,0:T(8,128)(2,1)}, u32[]{:S(2)}) copy-start(bf16[256,256]{1,0:T(8,128)(2,1)} %refs_5_.3) | copy-start | bytes 393220
  0.0 25.8 %copy-start.2 = (bf16[256,256]{1,0:T(8,128)(2,1)S(1)}, bf16[256,256]{1,0:T(8,128)(2,1)}, u32[]{:S(2)}) copy-start(bf16[256,256]{1,0:T(8,128)(2,1)} %refs_6_.3) | copy-start | bytes 393220
  0.0 25.8 %copy-start.3 = (f32[3,256]{1,0:T(4,128)S(1)}, f32[3,256]{1,0:T(4,128)}, u32[]{:S(2)}) copy-start(f32[3,256]{1,0:T(4,128)} %refs_7_.1) | copy-start | bytes 9220
  0.0 25.8 %collective-permute-start = (f32[3,2,256,256]{3,2,1,0:T(8,128)}, f32[3,2,256,256]{3,2,1,0:T(8,128)S(1)}, u32[]{:S(2)}, u32[]{:S(2)}) collective-permute-start(f32[3,2,256,256]{3,2,1,0:T(8,128)} %bitcast.10), channel_id=1, source_target_pairs={{0,8},{9,1},{2,10},{11,3},{4,12},{13,5},{6,14},{15,7},{16,24},{25,... | collective-permute-start | bytes 4718600 | tf_op jit(solution)/shard_map/ppermute | solution.py:140
  1.5 24.4 %collective-permute-start.3 = (f32[3,2,256,256]{3,2,1,0:T(8,128)}, f32[3,2,256,256]{3,2,1,0:T(8,128)S(1)}, u32[]{:S(2)}, u32[]{:S(2)}) collective-permute-start(f32[3,2,256,256]{3,2,1,0:T(8,128)} %bitcast.11), channel_id=1, source_target_pairs={{2,8},{15,1},{4,10},{9,3},{6,12},{11,5},{0,14},{13,7},{18,24},{31,... | collective-permute-start | bytes 4718600 | tf_op jit(solution)/shard_map/ppermute | solution.py:140
  4.1 16.1 %collective-permute-start.1 = (f32[2,2,256,256]{3,2,1,0:T(8,128)S(1)}, f32[2,2,256,256]{3,2,1,0:T(8,128)S(1)}, u32[]{:S(2)}, u32[]{:S(2)}) collective-permute-start(f32[2,2,256,256]{3,2,1,0:T(8,128)S(1)} %slice_bitcast_fusion), channel_id=1, source_target_pairs={{8,1},{1,8},{10,3},{3,10},{12,5},{5,12},{14,7},{7,14},{24,17},{17,... | collective-permute-start | bytes 3145736 | tf_op jit(solution)/shard_map/ppermute | solution.py:140
  6.0 19.8 %collective-permute-start.2 = (f32[1,2,256,256]{3,2,1,0:T(8,128)S(1)}, f32[1,2,256,256]{3,2,1,0:T(8,128)S(1)}, u32[]{:S(2)}, u32[]{:S(2)}) collective-permute-start(f32[1,2,256,256]{3,2,1,0:T(8,128)S(1)} %slice_bitcast_fusion.1), channel_id=1, source_target_pairs={{8,1},{1,8},{10,3},{3,10},{12,5},{5,12},{14,7},{7,14},{24,17},{17,... | collective-permute-start | bytes 1572872 | tf_op jit(solution)/shard_map/ppermute | solution.py:140
  20.2 21.3 %collective-permute-start.5 = (f32[2,2,256,256]{3,2,1,0:T(8,128)S(1)}, f32[2,2,256,256]{3,2,1,0:T(8,128)S(1)}, u32[]{:S(2)}, u32[]{:S(2)}) collective-permute-start(f32[2,2,256,256]{3,2,1,0:T(8,128)S(1)} %collective-permute-done.1.refs_1_), channel_id=1, source_target_pairs={{8,0},{1,9},{10,2},{3,11},{12,4},{5,13},{14,6},{7,15},{24,16},{17,... | collective-permute-start | bytes 3145736 | tf_op jit(solution)/shard_map/ppermute | solution.py:140
  21.5 19.9 %collective-permute-start.7 = (f32[2,2,256,256]{3,2,1,0:T(8,128)S(1)}, f32[2,2,256,256]{3,2,1,0:T(8,128)S(1)}, u32[]{:S(2)}, u32[]{:S(2)}) collective-permute-start(f32[2,2,256,256]{3,2,1,0:T(8,128)S(1)} %collective-permute-done.1.refs_1_), channel_id=1, source_target_pairs={{8,2},{1,15},{10,4},{3,9},{12,6},{5,11},{14,0},{7,13},{24,18},{17,... | collective-permute-start | bytes 3145736 | tf_op jit(solution)/shard_map/ppermute | solution.py:140
  30.2 15.5 %copy-start.4 = (f32[1,2,256,256]{3,2,1,0:T(8,128)}, f32[1,2,256,256]{3,2,1,0:T(8,128)S(1)}, u32[]{:S(2)}) copy-start(f32[1,2,256,256]{3,2,1,0:T(8,128)S(1)} %get-tuple-element.40) | copy-start | bytes 1572868
  30.2 27.2 %collective-permute-start.4 = (f32[3,2,256,256]{3,2,1,0:T(8,128)S(1)}, f32[3,2,256,256]{3,2,1,0:T(8,128)}, u32[]{:S(2)}, u32[]{:S(2)}) collective-permute-start(f32[3,2,256,256]{3,2,1,0:T(8,128)S(1)} %get-tuple-element.35), channel_id=1, source_target_pairs={{8,1},{1,8},{10,3},{3,10},{12,5},{5,12},{14,7},{7,14},{24,17},{17,... | collective-permute-start | bytes 4718600 | tf_op jit(solution)/shard_map/ppermute | solution.py:140
  32.2 2.8 %collective-permute-start.6 = (f32[1,2,256,256]{3,2,1,0:T(8,128)S(1)}, f32[1,2,256,256]{3,2,1,0:T(8,128)S(1)}, u32[]{:S(2)}, u32[]{:S(2)}) collective-permute-start(f32[1,2,256,256]{3,2,1,0:T(8,128)S(1)} %collective-permute-done.2.refs_2_), channel_id=1, source_target_pairs={{8,0},{1,9},{10,2},{3,11},{12,4},{5,13},{14,6},{7,15},{24,16},{17,... | collective-permute-start | bytes 1572872 | tf_op jit(solution)/shard_map/ppermute | solution.py:140
  33.5 8.0 %collective-permute-start.8 = (f32[1,2,256,256]{3,2,1,0:T(8,128)S(1)}, f32[1,2,256,256]{3,2,1,0:T(8,128)S(1)}, u32[]{:S(2)}, u32[]{:S(2)}) collective-permute-start(f32[1,2,256,256]{3,2,1,0:T(8,128)S(1)} %collective-permute-done.2.refs_2_), channel_id=1, source_target_pairs={{8,2},{1,15},{10,4},{3,9},{12,6},{5,11},{14,0},{7,13},{24,18},{17,... | collective-permute-start | bytes 1572872 | tf_op jit(solution)/shard_map/ppermute | solution.py:140
  35.0 24.1 %collective-permute-start.10 = (f32[2,2,256,256]{3,2,1,0:T(8,128)}, f32[2,2,256,256]{3,2,1,0:T(8,128)}, u32[]{:S(2)}, u32[]{:S(2)}) collective-permute-start(f32[2,2,256,256]{3,2,1,0:T(8,128)} %get-tuple-element.38), channel_id=1, source_target_pairs={{8,9},{1,16},{10,11},{3,18},{12,13},{5,20},{14,15},{7,22},{24,25},... | collective-permute-start | bytes 3145736 | tf_op jit(solution)/shard_map/ppermute | solution.py:140
  45.7 0.8 %copy-start.5 = (f32[1,2,256,256]{3,2,1,0:T(8,128)}, f32[1,2,256,256]{3,2,1,0:T(8,128)S(1)}, u32[]{:S(2)}) copy-start(f32[1,2,256,256]{3,2,1,0:T(8,128)S(1)} %get-tuple-element.39) | copy-start | bytes 1572868
  46.5 26.5 %collective-permute-start.9 = (f32[2,2,256,256]{3,2,1,0:T(8,128)}, f32[2,2,256,256]{3,2,1,0:T(8,128)}, u32[]{:S(2)}, u32[]{:S(2)}) collective-permute-start(f32[2,2,256,256]{3,2,1,0:T(8,128)} %get-tuple-element.37), channel_id=1, source_target_pairs={{0,8},{9,17},{2,10},{11,19},{4,12},{13,21},{6,14},{15,23},{16,24},... | collective-permute-start | bytes 3145736 | tf_op jit(solution)/shard_map/ppermute | solution.py:140
  47.8 27.9 %collective-permute-start.12 = (f32[1,2,256,256]{3,2,1,0:T(8,128)}, f32[1,2,256,256]{3,2,1,0:T(8,128)S(1)}, u32[]{:S(2)}, u32[]{:S(2)}) collective-permute-start(f32[1,2,256,256]{3,2,1,0:T(8,128)} %copy-done.4), channel_id=1, source_target_pairs={{8,9},{1,16},{10,11},{3,18},{12,13},{5,20},{14,15},{7,22},{24,25},... | collective-permute-start | bytes 1572872 | tf_op jit(solution)/shard_map/ppermute | solution.py:140
  56.2 22.3 %collective-permute-start.11 = (f32[1,2,256,256]{3,2,1,0:T(8,128)}, f32[1,2,256,256]{3,2,1,0:T(8,128)S(1)}, u32[]{:S(2)}, u32[]{:S(2)}) collective-permute-start(f32[1,2,256,256]{3,2,1,0:T(8,128)} %copy-done.5), channel_id=1, source_target_pairs={{0,8},{9,17},{2,10},{11,19},{4,12},{13,21},{6,14},{15,23},{16,24},... | collective-permute-start | bytes 1572872 | tf_op jit(solution)/shard_map/ppermute | solution.py:140

commit v3 on v2

v3 whole, which is shorter than its diff:
```python
import functools

import jax
import jax.numpy as jnp
from jax import lax
from jax.experimental import pallas as pl
from jax.experimental.pallas import tpu as pltpu
from jax.sharding import PartitionSpec as P


AXES = ("tm", "space")
STEP = 0.2
EARLY = 2


def routes(slices, slabs):
    at = lambda s, p: s * slabs + p % slabs
    cells = [(k, x, l) for k in range(slices // 2) for x in range(slabs // 2) for l in range(2)]
    side = lambda l: 1 - 2 * l
    stay = lambda k, x, l: at(2 * k + l, 2 * x + l)
    move = lambda k, x, l: at(2 * k + 1 - l, 2 * x + l)
    return {
        "swap": [(move(k, x, l), move(k, x, 1 - l)) for k, x, l in cells],
        "near_in": [(stay(k, x, l), move(k, x, l)) for k, x, l in cells],
        "far_in": [(stay(k, x + side(l), l), move(k, x, l)) for k, x, l in cells],
        "near_out": [(move(k, x, l), stay(k, x, l)) for k, x, l in cells],
        "far_out": [(move(k, x, l), stay(k, x + side(l), l)) for k, x, l in cells],
        "next_move": [
            (move(k, x, l), at(2 * k + l + 1, 2 * x + 1 - l)) for k, x, l in cells if 2 * k + l + 1 < slices
        ],
        "next_stay": [(stay(k, x, l), at(2 * k + l + 1, 2 * x + l)) for k, x, l in cells if 2 * k + l + 1 < slices],
    }


def advance(sizes, which, movers, *refs):
    mover = lax.axis_index(AXES[0]) % 2 != lax.axis_index(AXES[1]) % 2
    pl.when(mover == movers)(lambda: advance_plane(sizes, which, *refs))


def advance_plane(sizes, which, *refs):
    pieces, refs = refs[: sum(map(len, sizes))], refs[sum(map(len, sizes)) :]
    wall, span, base, a_out, b_out, mid, flow = refs
    slice_at, slab_at = lax.axis_index(AXES[0]), lax.axis_index(AXES[1])
    low = slice_at % 2
    lead = jnp.where((slice_at < 2) & (slab_at % 2 == 0), 1.0, 0.0).astype(jnp.float32)
    half = jnp.where(low == 1, 0.5, -0.5).astype(jnp.float32)

    def load(i):
        first_piece = sum(map(len, sizes[: i // 2]))
        entries = [(first_piece + n, c) for n, size in enumerate(sizes[i // 2]) for c in range(size)]
        slot = jnp.where(low == 1, i % 2, 1 - i % 2)
        return lambda c: pieces[entries[c][0]][entries[c][1], slot]

    for c in range(3):
        rows = jnp.broadcast_to(base[c : c + 1], (8, base.shape[1]))
        flow[c] = jnp.broadcast_to(rows.T[:, :1], flow.shape[1:])

    def slope(before, here, after):
        fields = [here(c) for c in range(3)]
        vx, vy, vz = [jnp.concatenate([flow[c]] * 2, axis=1) + fields[c] for c in range(3)]
        vx = vx * half
        for c in range(3):
            rounded = fields[c].astype(jnp.bfloat16)
            gy = jnp.dot(wall[...], rounded, preferred_element_type=jnp.float32)
            gz = jnp.dot(rounded, span[...], preferred_element_type=jnp.float32)
            yield fields[c], vx * (after(c) - before(c)) + vy * gy + vz * gz

    for n in range(3):
        i = which + n + 1
        for c, (u0, g0) in enumerate(slope(load(i - 1), load(i), load(i + 1))):
            u1 = u0 - STEP * g0
            mid[c, n] = u1
            if n == 1:
                b_out[c] = g0 * (0.5 * STEP) + lead * u1
    for c, (u1, g1) in enumerate(slope(*[lambda c, n=n: mid[c, n] for n in range(3)])):
        b_out[c] = b_out[c] - (0.5 * STEP) * g1
        a_out[c] = u1 - STEP * g1


def evaluate(slabs, which, movers, wall, span, base):
    sizes = [[piece.shape[0] for piece in slab] for slab in slabs]
    pieces = [piece for slab in slabs for piece in slab]
    ys, zs = pieces[0].shape[2:]
    shape = jax.ShapeDtypeStruct((3, ys, zs), jnp.float32)
    vmem = pl.BlockSpec(memory_space=pltpu.VMEM)
    return pl.pallas_call(
        functools.partial(advance, sizes, which, movers),
        out_shape=(shape, shape),
        in_specs=[vmem] * (len(pieces) + 3),
        out_specs=(vmem, vmem),
        scratch_shapes=[
            pltpu.VMEM((3, 3, ys, zs), jnp.float32),
            pltpu.VMEM((3, ys, zs // 2), jnp.float32),
        ],
        compiler_params=pltpu.CompilerParams(vmem_limit_bytes=12 * 2**20),
        cost_estimate=pl.CostEstimate(flops=24 * 2 * ys * ys * zs, bytes_accessed=21 * ys * zs * 4, transcendentals=0),
        name="advance",
    )(*pieces, wall, span, base)


def finish(which, *refs):
    back, b_stay, stay, move, out, first, second, sems = refs[-8:]
    slice_at, slab_at = lax.axis_index(AXES[0]), lax.axis_index(AXES[1])
    mover = slice_at % 2 != slab_at % 2
    slot = jnp.where(slab_at % 2 == 1, which, 1 - which)
    parts = range(first.shape[0])
    copies = lambda one, two: [
        (
            pltpu.make_async_copy(one.at[c], first.at[c], sems.at[0, c]),
            pltpu.make_async_copy(two.at[c], second.at[c], sems.at[1, c]),
        )
        for c in parts
    ]

    def start(one, two):
        for pair in copies(one, two):
            for copy in pair:
                copy.start()

    pl.when(mover)(lambda: start(back, stay))
    pl.when(jnp.logical_not(mover))(lambda: start(b_stay, move))
    writes = []
    for c, pair in enumerate(copies(back, stay)):
        for copy in pair:
            copy.wait()
        first[c] = first[c] + second[c]
        writes.append(pltpu.make_async_copy(first.at[c], out.at[c, slot], sems.at[2, c]))
        writes[-1].start()
    for write in writes:
        write.wait()


def combine(result, which, *parts):
    shape = parts[0].shape
    any_space = pl.BlockSpec(memory_space=pl.ANY)
    operands = parts if result is None else (result, *parts)
    return pl.pallas_call(
        functools.partial(finish, which),
        out_shape=jax.ShapeDtypeStruct((shape[0], 2, *shape[1:]), jnp.float32),
        in_specs=[any_space] * len(operands),
        out_specs=any_space,
        input_output_aliases={} if result is None else {0: 0},
        scratch_shapes=[
            pltpu.VMEM(shape, jnp.float32),
            pltpu.VMEM(shape, jnp.float32),
            pltpu.SemaphoreType.DMA((3, shape[0])),
        ],
        compiler_params=pltpu.CompilerParams(vmem_limit_bytes=4 * 2**20),
        name="finish",
    )(*operands)


def local(ways, start_states, wall_normal, spanwise, base_flow):
    home = start_states[0]
    step = functools.partial(evaluate, wall=wall_normal, span=spanwise, base=base_flow)

    def send(what, way):
        return lax.ppermute(what, AXES, ways[way])

    far_in = send(home, "far_in")
    own_early = send(home[:EARLY], "swap")
    own_late = send(home[EARLY:], "swap")
    near_in = send(home, "near_in")
    far_early = send(own_early, "far_out")
    near_early = send(own_early, "near_out")
    slabs = [[near_in], [own_early, own_late], [far_in]]
    a_move_0, b_move_0 = step(slabs, 0, True)
    back_0 = send(b_move_0, "swap")
    move_0 = send(a_move_0, "next_move")
    far_late = send(own_late, "far_out")
    near_late = send(own_late, "near_out")
    a_move_1, b_move_1 = step(slabs, 1, True)
    back_1 = send(b_move_1, "swap")
    move_1 = send(a_move_1, "next_move")
    slabs = [[near_early, near_late], [home], [far_early, far_late]]
    a_stay_0, b_stay_0 = step(slabs, 0, False)
    stay_0 = send(a_stay_0, "next_stay")
    a_stay_1, b_stay_1 = step(slabs, 1, False)
    stay_1 = send(a_stay_1, "next_stay")
    result = combine(None, 0, back_0, b_stay_0, stay_0, move_0)
    return combine(result, 1, back_1, b_stay_1, stay_1, move_1)[None]


def solution(mesh):
    placed = (P("tm", None, "space", None, None), P(), P(), P())
    ways = routes(mesh.shape["tm"], mesh.shape["space"])
    return jax.shard_map(
        functools.partial(local, ways),
        mesh=mesh,
        in_specs=placed,
        out_specs=P("tm", None, "space", None, None),
        check_vma=False,
    )
```

time: 79.8 us -> 86.2 us (1.080)
  waiting for transfers between devices: 30.9 us -> 50.9 us
  starting transfers between devices: 32.2 us -> 26.5 us
  other arithmetic: 4.15 us -> 0 us
  local copies, waits for them, and re-layouts: 3.31 us -> 1.35 us
  Pallas kernels: 8.58 us -> 6.78 us
    ppermute x13 -> x14, waiting for transfers between devices: 30.9 us -> 50.9 us  [send(): return lax.ppermute(what, AXES, ways[way])]
    ppermute x13 -> x14, starting transfers between devices: 32.2 us -> 26.5 us  [send(): return lax.ppermute(what, AXES, ways[way])]
    scatter-add x2 -> x0, other arithmetic: 2.53 us -> none  [the longest x1 1.63 us: local(): result = result.at[:EARLY].add(jnp.where(mover, stay_early, move_early))]
    unnamed x13 -> x8, local copies, waits for them, and re-layouts: 1.97 us -> 0.02 us
    pallas_call x2 -> x6, Pallas kernels: 8.58 us -> 6.78 us  [the longest x4 4.59 us: evaluate(): pl.pallas_call(functools.partial(advance, sizes, which, movers), out_shap...]
    select_n x1 -> x0, other arithmetic: 1.62 us -> none  [local(): result = jnp.where(mover, back, b_stay)]
  transfers between devices with their start and end apart: 13 -> 14, of which waited for: 6 -> 6; matrix products, arithmetic and copies ran while one was open for 7% -> 2% of each run, Pallas kernels for 11% -> 7%
where the time goes in v3:
time: 86.2 us; the launch traced here: 85.8 us
  waiting for transfers between devices  50.9 us (59%)
  starting transfers between devices  26.5 us (31%)
  Pallas kernels  6.78 us (8%)
  local copies, waits for them, and re-layouts  1.35 us (2%)
    ppermute x14, waiting for transfers between devices, send(): return lax.ppermute(what, AXES, ways[way])  50.9 us
    ppermute x14, starting transfers between devices, send(): return lax.ppermute(what, AXES, ways[way])  26.5 us
    pallas_call x4, Pallas kernels, evaluate(): pl.pallas_call(functools.partial(advance, sizes, which, movers), out_shap...  4.59 us
    pallas_call x2, Pallas kernels, combine(): pl.pallas_call(functools.partial(finish, which), out_shape=jax.ShapeDtype...  2.19 us
  transfers between devices with their start and end apart: 14, of which 6 were waited for; matrix products, arithmetic and copies ran while one was open for 2% of the time, Pallas kernels for 7%

profile of v3, /device:TPU:136, one launch (start us, length us, event | category | flops | bytes accessed | tf_op | source)
XLA Modules:
  0.0 85.8 jit_solution(6558415887689274913)
XLA Ops:
  0.0 1.4 %collective-permute-start.3 = (f32[3,2,256,256]{3,2,1,0:T(8,128)}, f32[3,2,256,256]{3,2,1,0:T(8,128)S(1)}, u32[]{:S(2)}, u32[]{:S(2)}) collective-permute-start(f32[3,2,256,256]{3,2,1,0:T(8,128)} %bitcast.6), channel_id=1, source_target_pairs={{2,8},{15,1},{4,10},{9,3},{6,12},{11,5},{0,14},{13,7},{18,24},{31,... | collective-permute-start | bytes 4718600 | tf_op jit(solution)/shard_map/ppermute | solution.py:158
  1.5 1.3 %collective-permute-start = (f32[3,2,256,256]{3,2,1,0:T(8,128)}, f32[3,2,256,256]{3,2,1,0:T(8,128)S(1)}, u32[]{:S(2)}, u32[]{:S(2)}) collective-permute-start(f32[3,2,256,256]{3,2,1,0:T(8,128)} %bitcast.7), channel_id=1, source_target_pairs={{0,8},{9,1},{2,10},{11,3},{4,12},{13,5},{6,14},{15,7},{16,24},{25,... | collective-permute-start | bytes 4718600 | tf_op jit(solution)/shard_map/ppermute | solution.py:158
  2.8 1.3 %slice_bitcast_fusion = f32[2,2,256,256]{3,2,1,0:T(8,128)S(1)} fusion(f32[1,3,2,256,256]{4,3,2,1,0:T(8,128)} %param.4), kind=kLoop, calls=%fused_computation | loop fusion | bytes 2097152 | tf_op jit(solution)/shard_map/slice | solution.py:161
  4.1 1.9 %collective-permute-start.1 = (f32[2,2,256,256]{3,2,1,0:T(8,128)S(1)}, f32[2,2,256,256]{3,2,1,0:T(8,128)S(1)}, u32[]{:S(2)}, u32[]{:S(2)}) collective-permute-start(f32[2,2,256,256]{3,2,1,0:T(8,128)S(1)} %slice_bitcast_fusion), channel_id=1, source_target_pairs={{8,1},{1,8},{10,3},{3,10},{12,5},{5,12},{14,7},{7,14},{24,17},{17,... | collective-permute-start | bytes 3145736 | tf_op jit(solution)/shard_map/ppermute | solution.py:158
  6.0 3.6 %collective-permute-start.2 = (f32[1,2,256,256]{3,2,1,0:T(8,128)S(1)}, f32[1,2,256,256]{3,2,1,0:T(8,128)S(1)}, u32[]{:S(2)}, u32[]{:S(2)}) collective-permute-start(f32[1,2,256,256]{3,2,1,0:T(8,128)S(1)} %slice_bitcast_fusion.1), channel_id=1, source_target_pairs={{8,1},{1,8},{10,3},{3,10},{12,5},{5,12},{14,7},{7,14},{24,17},{17,... | collective-permute-start | bytes 1572872 | tf_op jit(solution)/shard_map/ppermute | solution.py:158
  9.7 10.5 %collective-permute-done.1.refs_1_ = f32[2,2,256,256]{3,2,1,0:T(8,128)S(1)} collective-permute-done((f32[2,2,256,256]{3,2,1,0:T(8,128)S(1)}, f32[2,2,256,256]{3,2,1,0:T(8,128)S(1)}, u32[]{:S(2)}, u32[]{:S(2)}) %collective-permute-start.1) | collective-permute-done | bytes 1048608 | tf_op jit(solution)/shard_map/ppermute | solution.py:158
  20.2 1.3 %collective-permute-start.7 = (f32[2,2,256,256]{3,2,1,0:T(8,128)S(1)}, f32[2,2,256,256]{3,2,1,0:T(8,128)S(1)}, u32[]{:S(2)}, u32[]{:S(2)}) collective-permute-start(f32[2,2,256,256]{3,2,1,0:T(8,128)S(1)} %collective-permute-done.1.refs_1_), channel_id=1, source_target_pairs={{8,2},{1,15},{10,4},{3,9},{12,6},{5,11},{14,0},{7,13},{24,18},{17,... | collective-permute-start | bytes 3145736 | tf_op jit(solution)/shard_map/ppermute | solution.py:158
  21.5 1.4 %collective-permute-start.5 = (f32[2,2,256,256]{3,2,1,0:T(8,128)S(1)}, f32[2,2,256,256]{3,2,1,0:T(8,128)S(1)}, u32[]{:S(2)}, u32[]{:S(2)}) collective-permute-start(f32[2,2,256,256]{3,2,1,0:T(8,128)S(1)} %collective-permute-done.1.refs_1_), channel_id=1, source_target_pairs={{8,0},{1,9},{10,2},{3,11},{12,4},{5,13},{14,6},{7,15},{24,16},{17,... | collective-permute-start | bytes 3145736 | tf_op jit(solution)/shard_map/ppermute | solution.py:158
  22.9 2.9 %collective-permute-done.2.refs_2_ = f32[1,2,256,256]{3,2,1,0:T(8,128)S(1)} collective-permute-done((f32[1,2,256,256]{3,2,1,0:T(8,128)S(1)}, f32[1,2,256,256]{3,2,1,0:T(8,128)S(1)}, u32[]{:S(2)}, u32[]{:S(2)}) %collective-permute-start.2) | collective-permute-done | bytes 524320 | tf_op jit(solution)/shard_map/ppermute | solution.py:158
  25.8 0.0 collective-permute-done.3.refs_3_
  25.8 0.0 collective-permute-done.refs_0_
  25.8 2.3 %advance.4 = (f32[3,256,256]{2,1,0:T(8,128)S(1)}, f32[3,256,256]{2,1,0:T(8,128)S(1)}) custom-call(f32[3,2,256,256]{3,2,1,0:T(8,128)S(1)} %collective-permute-done.refs_0_, f32[2,2,256,256]{3,2,1,0:T(8,128)S(1)} %collective-permute-done.1.refs_1_, f32[1,2,256,256]{3,2,1,0:T(8,128)S(1)} %collective-permute-done.2.refs_2_, ...), custom_call_target="tpu_custom_call" | custom-call | flops 805306368 | bytes 5505024 | tf_op jit(solution)/shard_map/advance/pallas_call | solution.py:86
  28.1 2.2 %collective-permute-start.4 = (f32[3,256,256]{2,1,0:T(8,128)S(1)}, f32[3,256,256]{2,1,0:T(8,128)S(1)}, u32[]{:S(2)}, u32[]{:S(2)}) collective-permute-start(f32[3,256,256]{2,1,0:T(8,128)S(1)} %get-tuple-element.13), channel_id=1, source_target_pairs={{8,1},{1,8},{10,3},{3,10},{12,5},{5,12},{14,7},{7,14},{24,17},{17,... | collective-permute-start | bytes 2359304 | tf_op jit(solution)/shard_map/ppermute | solution.py:158
  30.3 1.3 %collective-permute-start.8 = (f32[1,2,256,256]{3,2,1,0:T(8,128)S(1)}, f32[1,2,256,256]{3,2,1,0:T(8,128)S(1)}, u32[]{:S(2)}, u32[]{:S(2)}) collective-permute-start(f32[1,2,256,256]{3,2,1,0:T(8,128)S(1)} %collective-permute-done.2.refs_2_), channel_id=1, source_target_pairs={{8,2},{1,15},{10,4},{3,9},{12,6},{5,11},{14,0},{7,13},{24,18},{17,... | collective-permute-start | bytes 1572872 | tf_op jit(solution)/shard_map/ppermute | solution.py:158
  31.7 1.3 %collective-permute-start.6 = (f32[1,2,256,256]{3,2,1,0:T(8,128)S(1)}, f32[1,2,256,256]{3,2,1,0:T(8,128)S(1)}, u32[]{:S(2)}, u32[]{:S(2)}) collective-permute-start(f32[1,2,256,256]{3,2,1,0:T(8,128)S(1)} %collective-permute-done.2.refs_2_), channel_id=1, source_target_pairs={{8,0},{1,9},{10,2},{3,11},{12,4},{5,13},{14,6},{7,15},{24,16},{17,... | collective-permute-start | bytes 1572872 | tf_op jit(solution)/shard_map/ppermute | solution.py:158
  33.0 2.3 %advance.6 = (f32[3,256,256]{2,1,0:T(8,128)S(1)}, f32[3,256,256]{2,1,0:T(8,128)S(1)}) custom-call(f32[3,2,256,256]{3,2,1,0:T(8,128)S(1)} %collective-permute-done.refs_0_, f32[2,2,256,256]{3,2,1,0:T(8,128)S(1)} %collective-permute-done.1.refs_1_, f32[1,2,256,256]{3,2,1,0:T(8,128)S(1)} %collective-permute-done.2.refs_2_, ...), custom_call_target="tpu_custom_call" | custom-call | flops 805306368 | bytes 5505024 | tf_op jit(solution)/shard_map/advance/pallas_call | solution.py:86
  35.3 4.1 %collective-permute-done.8.refs_4_ = f32[1,2,256,256]{3,2,1,0:T(8,128)S(1)} collective-permute-done((f32[1,2,256,256]{3,2,1,0:T(8,128)S(1)}, f32[1,2,256,256]{3,2,1,0:T(8,128)S(1)}, u32[]{:S(2)}, u32[]{:S(2)}) %collective-permute-start.8) | collective-permute-done | bytes 524320 | tf_op jit(solution)/shard_map/ppermute | solution.py:158
  39.4 1.9 %collective-permute-start.11 = (f32[3,256,256]{2,1,0:T(8,128)S(1)}, f32[3,256,256]{2,1,0:T(8,128)S(1)}, u32[]{:S(2)}, u32[]{:S(2)}) collective-permute-start(f32[3,256,256]{2,1,0:T(8,128)S(1)} %get-tuple-element.17), channel_id=1, source_target_pairs={{8,1},{1,8},{10,3},{3,10},{12,5},{5,12},{14,7},{7,14},{24,17},{17,... | collective-permute-start | bytes 2359304 | tf_op jit(solution)/shard_map/ppermute | solution.py:158
  41.3 0.0 collective-permute-done.6.refs_1_
  41.3 4.9 %collective-permute-start.13 = (f32[3,256,256]{2,1,0:T(8,128)S(1)}, f32[3,256,256]{2,1,0:T(8,128)S(1)}, u32[]{:S(2)}, u32[]{:S(2)}) collective-permute-start(f32[3,256,256]{2,1,0:T(8,128)S(1)} %get-tuple-element.20), channel_id=1, source_target_pairs={{8,9},{1,16},{10,11},{3,18},{12,13},{5,20},{14,15},{7,22},{24,25},... | collective-permute-start | bytes 2359304 | tf_op jit(solution)/shard_map/ppermute | solution.py:158
  46.2 0.0 collective-permute-done.7.refs_3_
  46.2 1.3 %collective-permute-start.10 = (f32[3,256,256]{2,1,0:T(8,128)S(1)}, f32[3,256,256]{2,1,0:T(8,128)S(1)}, u32[]{:S(2)}, u32[]{:S(2)}) collective-permute-start(f32[3,256,256]{2,1,0:T(8,128)S(1)} %get-tuple-element.16), channel_id=1, source_target_pairs={{8,9},{1,16},{10,11},{3,18},{12,13},{5,20},{14,15},{7,22},{24,25},... | collective-permute-start | bytes 2359304 | tf_op jit(solution)/shard_map/ppermute | solution.py:158
  47.5 0.0 collective-permute-done.5.refs_0_
  47.6 1.3 %collective-permute-start.9 = (f32[3,256,256]{2,1,0:T(8,128)S(1)}, f32[3,256,256]{2,1,0:T(8,128)S(1)}, u32[]{:S(2)}, u32[]{:S(2)}) collective-permute-start(f32[3,256,256]{2,1,0:T(8,128)S(1)} %get-tuple-element.15), channel_id=1, source_target_pairs={{0,8},{9,17},{2,10},{11,19},{4,12},{13,21},{6,14},{15,23},{16,24},... | collective-permute-start | bytes 2359304 | tf_op jit(solution)/shard_map/ppermute | solution.py:158
  48.9 0.0 collective-permute-done.4.refs_0_
  48.9 1.3 %collective-permute-start.12 = (f32[3,256,256]{2,1,0:T(8,128)S(1)}, f32[3,256,256]{2,1,0:T(8,128)S(1)}, u32[]{:S(2)}, u32[]{:S(2)}) collective-permute-start(f32[3,256,256]{2,1,0:T(8,128)S(1)} %get-tuple-element.19), channel_id=1, source_target_pairs={{0,8},{9,17},{2,10},{11,19},{4,12},{13,21},{6,14},{15,23},{16,24},... | collective-permute-start | bytes 2359304 | tf_op jit(solution)/shard_map/ppermute | solution.py:158
  50.2 13.8 %collective-permute-done.10.refs_3_ = f32[3,256,256]{2,1,0:T(8,128)S(1)} collective-permute-done((f32[3,256,256]{2,1,0:T(8,128)S(1)}, f32[3,256,256]{2,1,0:T(8,128)S(1)}, u32[]{:S(2)}, u32[]{:S(2)}) %collective-permute-start.10) | collective-permute-done | bytes 786464 | tf_op jit(solution)/shard_map/ppermute | solution.py:158
  64.0 8.9 %collective-permute-done.9.refs_2_ = f32[3,256,256]{2,1,0:T(8,128)S(1)} collective-permute-done((f32[3,256,256]{2,1,0:T(8,128)S(1)}, f32[3,256,256]{2,1,0:T(8,128)S(1)}, u32[]{:S(2)}, u32[]{:S(2)}) %collective-permute-start.9) | collective-permute-done | bytes 786464 | tf_op jit(solution)/shard_map/ppermute | solution.py:158
  72.9 1.1 %finish.2.refs_0_ = f32[3,2,256,256]{3,2,1,0:T(8,128)} custom-call(f32[3,256,256]{2,1,0:T(8,128)S(1)} %collective-permute-done.4.refs_0_, f32[3,256,256]{2,1,0:T(8,128)S(1)} %get-tuple-element.14.refs_1_, f32[3,256,256]{2,1,0:T(8,128)S(1)} %collective-permute-done.9.refs_2_, f32[3,256,256]{2,1,0:T(8,128)S(1)} %collective-permute-done.10.refs_3_), custom_call_target="tpu_custom_call" | custom-call | tf_op jit(solution)/shard_map/finish/pallas_call | solution.py:137
  74.0 0.0 collective-permute-done.11.refs_1_
  74.0 10.6 %collective-permute-done.12.refs_3_ = f32[3,256,256]{2,1,0:T(8,128)S(1)} collective-permute-done((f32[3,256,256]{2,1,0:T(8,128)S(1)}, f32[3,256,256]{2,1,0:T(8,128)S(1)}, u32[]{:S(2)}, u32[]{:S(2)}) %collective-permute-start.12) | collective-permute-done | bytes 786464 | tf_op jit(solution)/shard_map/ppermute | solution.py:158
  84.7 1.1 %finish.3 = f32[3,2,256,256]{3,2,1,0:T(8,128)} custom-call(f32[3,2,256,256]{3,2,1,0:T(8,128)} %finish.2.refs_0_, f32[3,256,256]{2,1,0:T(8,128)S(1)} %collective-permute-done.11.refs_1_, f32[3,256,256]{2,1,0:T(8,128)S(1)} %get-tuple-element.18.refs_2_, f32[3,256,256]{2,1,0:T(8,128)S(1)} %collective-permute-done.12.refs_3_, ...), custom_call_target="tpu_custom_call", output_to_operand_aliasing={{}: (0, {})} | custom-call | tf_op jit(solution)/shard_map/finish/pallas_call | solution.py:137
  (12 shorter events, 0.1 us)
Async XLA Ops:
  0.0 6.0 %copy-start = (f32[1,3,2,256,256]{4,3,2,1,0:T(8,128)S(1)}, f32[1,3,2,256,256]{4,3,2,1,0:T(8,128)}, u32[]{:S(2)}) copy-start(f32[1,3,2,256,256]{4,3,2,1,0:T(8,128)} %param.4) | copy-start | bytes 4718596
  0.0 25.8 %copy-start.1 = (bf16[256,256]{1,0:T(8,128)(2,1)S(1)}, bf16[256,256]{1,0:T(8,128)(2,1)}, u32[]{:S(2)}) copy-start(bf16[256,256]{1,0:T(8,128)(2,1)} %refs_5_.7) | copy-start | bytes 393220
  0.0 25.8 %copy-start.2 = (bf16[256,256]{1,0:T(8,128)(2,1)S(1)}, bf16[256,256]{1,0:T(8,128)(2,1)}, u32[]{:S(2)}) copy-start(bf16[256,256]{1,0:T(8,128)(2,1)} %refs_6_.7) | copy-start | bytes 393220
  0.0 25.8 %copy-start.3 = (f32[3,256]{1,0:T(4,128)S(1)}, f32[3,256]{1,0:T(4,128)}, u32[]{:S(2)}) copy-start(f32[3,256]{1,0:T(4,128)} %refs_7_.3) | copy-start | bytes 9220
  0.0 25.8 %collective-permute-start.3 = (f32[3,2,256,256]{3,2,1,0:T(8,128)}, f32[3,2,256,256]{3,2,1,0:T(8,128)S(1)}, u32[]{:S(2)}, u32[]{:S(2)}) collective-permute-start(f32[3,2,256,256]{3,2,1,0:T(8,128)} %bitcast.6), channel_id=1, source_target_pairs={{2,8},{15,1},{4,10},{9,3},{6,12},{11,5},{0,14},{13,7},{18,24},{31,... | collective-permute-start | bytes 4718600 | tf_op jit(solution)/shard_map/ppermute | solution.py:158
  1.5 24.3 %collective-permute-start = (f32[3,2,256,256]{3,2,1,0:T(8,128)}, f32[3,2,256,256]{3,2,1,0:T(8,128)S(1)}, u32[]{:S(2)}, u32[]{:S(2)}) collective-permute-start(f32[3,2,256,256]{3,2,1,0:T(8,128)} %bitcast.7), channel_id=1, source_target_pairs={{0,8},{9,1},{2,10},{11,3},{4,12},{13,5},{6,14},{15,7},{16,24},{25,... | collective-permute-start | bytes 4718600 | tf_op jit(solution)/shard_map/ppermute | solution.py:158
  4.1 16.1 %collective-permute-start.1 = (f32[2,2,256,256]{3,2,1,0:T(8,128)S(1)}, f32[2,2,256,256]{3,2,1,0:T(8,128)S(1)}, u32[]{:S(2)}, u32[]{:S(2)}) collective-permute-start(f32[2,2,256,256]{3,2,1,0:T(8,128)S(1)} %slice_bitcast_fusion), channel_id=1, source_target_pairs={{8,1},{1,8},{10,3},{3,10},{12,5},{5,12},{14,7},{7,14},{24,17},{17,... | collective-permute-start | bytes 3145736 | tf_op jit(solution)/shard_map/ppermute | solution.py:158
  6.0 19.8 %collective-permute-start.2 = (f32[1,2,256,256]{3,2,1,0:T(8,128)S(1)}, f32[1,2,256,256]{3,2,1,0:T(8,128)S(1)}, u32[]{:S(2)}, u32[]{:S(2)}) collective-permute-start(f32[1,2,256,256]{3,2,1,0:T(8,128)S(1)} %slice_bitcast_fusion.1), channel_id=1, source_target_pairs={{8,1},{1,8},{10,3},{3,10},{12,5},{5,12},{14,7},{7,14},{24,17},{17,... | collective-permute-start | bytes 1572872 | tf_op jit(solution)/shard_map/ppermute | solution.py:158
  20.2 26.0 %collective-permute-start.7 = (f32[2,2,256,256]{3,2,1,0:T(8,128)S(1)}, f32[2,2,256,256]{3,2,1,0:T(8,128)S(1)}, u32[]{:S(2)}, u32[]{:S(2)}) collective-permute-start(f32[2,2,256,256]{3,2,1,0:T(8,128)S(1)} %collective-permute-done.1.refs_1_), channel_id=1, source_target_pairs={{8,2},{1,15},{10,4},{3,9},{12,6},{5,11},{14,0},{7,13},{24,18},{17,... | collective-permute-start | bytes 3145736 | tf_op jit(solution)/shard_map/ppermute | solution.py:158
  21.5 26.0 %collective-permute-start.5 = (f32[2,2,256,256]{3,2,1,0:T(8,128)S(1)}, f32[2,2,256,256]{3,2,1,0:T(8,128)S(1)}, u32[]{:S(2)}, u32[]{:S(2)}) collective-permute-start(f32[2,2,256,256]{3,2,1,0:T(8,128)S(1)} %collective-permute-done.1.refs_1_), channel_id=1, source_target_pairs={{8,0},{1,9},{10,2},{3,11},{12,4},{5,13},{14,6},{7,15},{24,16},{17,... | collective-permute-start | bytes 3145736 | tf_op jit(solution)/shard_map/ppermute | solution.py:158
  28.1 20.8 %collective-permute-start.4 = (f32[3,256,256]{2,1,0:T(8,128)S(1)}, f32[3,256,256]{2,1,0:T(8,128)S(1)}, u32[]{:S(2)}, u32[]{:S(2)}) collective-permute-start(f32[3,256,256]{2,1,0:T(8,128)S(1)} %get-tuple-element.13), channel_id=1, source_target_pairs={{8,1},{1,8},{10,3},{3,10},{12,5},{5,12},{14,7},{7,14},{24,17},{17,... | collective-permute-start | bytes 2359304 | tf_op jit(solution)/shard_map/ppermute | solution.py:158
  30.3 9.1 %collective-permute-start.8 = (f32[1,2,256,256]{3,2,1,0:T(8,128)S(1)}, f32[1,2,256,256]{3,2,1,0:T(8,128)S(1)}, u32[]{:S(2)}, u32[]{:S(2)}) collective-permute-start(f32[1,2,256,256]{3,2,1,0:T(8,128)S(1)} %collective-permute-done.2.refs_2_), channel_id=1, source_target_pairs={{8,2},{1,15},{10,4},{3,9},{12,6},{5,11},{14,0},{7,13},{24,18},{17,... | collective-permute-start | bytes 1572872 | tf_op jit(solution)/shard_map/ppermute | solution.py:158
  31.7 9.6 %collective-permute-start.6 = (f32[1,2,256,256]{3,2,1,0:T(8,128)S(1)}, f32[1,2,256,256]{3,2,1,0:T(8,128)S(1)}, u32[]{:S(2)}, u32[]{:S(2)}) collective-permute-start(f32[1,2,256,256]{3,2,1,0:T(8,128)S(1)} %collective-permute-done.2.refs_2_), channel_id=1, source_target_pairs={{8,0},{1,9},{10,2},{3,11},{12,4},{5,13},{14,6},{7,15},{24,16},{17,... | collective-permute-start | bytes 1572872 | tf_op jit(solution)/shard_map/ppermute | solution.py:158
  39.4 34.6 %collective-permute-start.11 = (f32[3,256,256]{2,1,0:T(8,128)S(1)}, f32[3,256,256]{2,1,0:T(8,128)S(1)}, u32[]{:S(2)}, u32[]{:S(2)}) collective-permute-start(f32[3,256,256]{2,1,0:T(8,128)S(1)} %get-tuple-element.17), channel_id=1, source_target_pairs={{8,1},{1,8},{10,3},{3,10},{12,5},{5,12},{14,7},{7,14},{24,17},{17,... | collective-permute-start | bytes 2359304 | tf_op jit(solution)/shard_map/ppermute | solution.py:158
  41.3 32.7 %collective-permute-start.13 = (f32[3,256,256]{2,1,0:T(8,128)S(1)}, f32[3,256,256]{2,1,0:T(8,128)S(1)}, u32[]{:S(2)}, u32[]{:S(2)}) collective-permute-start(f32[3,256,256]{2,1,0:T(8,128)S(1)} %get-tuple-element.20), channel_id=1, source_target_pairs={{8,9},{1,16},{10,11},{3,18},{12,13},{5,20},{14,15},{7,22},{24,25},... | collective-permute-start | bytes 2359304 | tf_op jit(solution)/shard_map/ppermute | solution.py:158
  46.2 17.9 %collective-permute-start.10 = (f32[3,256,256]{2,1,0:T(8,128)S(1)}, f32[3,256,256]{2,1,0:T(8,128)S(1)}, u32[]{:S(2)}, u32[]{:S(2)}) collective-permute-start(f32[3,256,256]{2,1,0:T(8,128)S(1)} %get-tuple-element.16), channel_id=1, source_target_pairs={{8,9},{1,16},{10,11},{3,18},{12,13},{5,20},{14,15},{7,22},{24,25},... | collective-permute-start | bytes 2359304 | tf_op jit(solution)/shard_map/ppermute | solution.py:158
  47.6 25.3 %collective-permute-start.9 = (f32[3,256,256]{2,1,0:T(8,128)S(1)}, f32[3,256,256]{2,1,0:T(8,128)S(1)}, u32[]{:S(2)}, u32[]{:S(2)}) collective-permute-start(f32[3,256,256]{2,1,0:T(8,128)S(1)} %get-tuple-element.15), channel_id=1, source_target_pairs={{0,8},{9,17},{2,10},{11,19},{4,12},{13,21},{6,14},{15,23},{16,24},... | collective-permute-start | bytes 2359304 | tf_op jit(solution)/shard_map/ppermute | solution.py:158
  48.9 35.8 %collective-permute-start.12 = (f32[3,256,256]{2,1,0:T(8,128)S(1)}, f32[3,256,256]{2,1,0:T(8,128)S(1)}, u32[]{:S(2)}, u32[]{:S(2)}) collective-permute-start(f32[3,256,256]{2,1,0:T(8,128)S(1)} %get-tuple-element.19), channel_id=1, source_target_pairs={{0,8},{9,17},{2,10},{11,19},{4,12},{13,21},{6,14},{15,23},{16,24},... | collective-permute-start | bytes 2359304 | tf_op jit(solution)/shard_map/ppermute | solution.py:158
